TPU v7x, 32 devices: a whole 2x2x4 slice. The times are simulated.
32 devices in a mesh: grid: 8 (over z, y), band: 4 (over x, core).
Axes of the slice: x: 2, y: 2, z: 4, core: 2. Of those that a mesh axis runs over, the one named last changes fastest.
Arguments:
- orbitals: float32 [32, 16, 16, 512], P('grid', None, None, 'band'), may hold values from -80 to 80
- projectors: float32 [32, 16, 16, 512], P('grid', None, None, 'band'), may hold values from -0.09375 to 0.09375
- potential: float32 [32, 16, 16], P('grid'), may hold values from 0.3 to 3
Outputs:
- updated_orbitals: float32 [32, 16, 16, 512], P('grid', None, None, 'band')
- rayleigh_quotients: float32 [3, 512], P(None, 'band')
- residual_norms: float32 [3, 512], P(None, 'band')
All inputs are finite; a program needn't handle non-finite values.
Results may differ from a plain program's by a relative error of at most 0.00012.
Values sent between devices are 32-bit elements; how exact they have to be, the bound alone decides.
A program may use at most 128 MiB of HBM per device.

v0:
```python
import jax
import jax.numpy as jnp
from jax import lax
from jax.sharding import PartitionSpec as P

ITERS = 3


STENCIL = (-205.0 / 72.0, 8.0 / 5.0, -1.0 / 5.0, 8.0 / 315.0, -1.0 / 560.0)
STEP_LENGTH = 0.25
NORM_EPS = 1e-06
HIGHEST = lax.Precision.HIGHEST


def with_halo(block, sides, width):
    for axis, dim in sides:
        count = lax.axis_size(axis)
        forward = [(i, i + 1) for i in range(count - 1)]
        forward.append((count - 1, 0))
        backward = [(target, source) for source, target in forward]
        low = lax.ppermute(
            lax.slice_in_dim(block, block.shape[dim] - width, None, axis=dim), axis, forward
        )
        high = lax.ppermute(lax.slice_in_dim(block, 0, width, axis=dim), axis, backward)
        block = jnp.concatenate([low, block, high], axis=dim)
    return block


def matmul(left, right):
    return jnp.dot(left, right, precision=HIGHEST, preferred_element_type=jnp.float32)


def laplacian(grid_field):
    padded = with_halo(grid_field, (("grid", 0),), 4)
    planes_here = grid_field.shape[0]
    result = 3.0 * STENCIL[0] * grid_field
    for distance in range(1, 5):
        result = result + STENCIL[distance] * (
            padded[4 + distance : 4 + distance + planes_here]
            + padded[4 - distance : 4 - distance + planes_here]
        )
    for dimension in (1, 2):
        for distance in range(1, 5):
            result = result + STENCIL[distance] * (
                jnp.roll(grid_field, distance, dimension)
                + jnp.roll(grid_field, -distance, dimension)
            )
    return result


def local(orbitals, projectors, potential):
    grid_shape = orbitals.shape
    local_bands = orbitals.shape[3]
    total_bands = local_bands * lax.axis_size("band")
    first_band = lax.axis_index("band") * local_bands
    vectors = orbitals.reshape(-1, local_bands)
    every_projector = lax.all_gather(projectors, "band", axis=3, tiled=True).reshape(
        -1, projectors.shape[3] * lax.axis_size("band")
    )
    identity_matrix = jnp.eye(total_bands, dtype=jnp.float32)
    quotient_list = []
    norm_list = []
    for iteration in range(ITERS):
        gathered = lax.all_gather(vectors.reshape(grid_shape), "band", axis=3, tiled=True).reshape(
            -1, total_bands
        )
        margin = lax.psum(matmul(gathered.T, gathered), "grid")
        factor = jnp.linalg.cholesky(margin)
        inverse = jax.scipy.linalg.solve_triangular(factor, identity_matrix, lower=True)
        transform = inverse.T
        vectors = matmul(gathered, lax.dynamic_slice_in_dim(transform, first_band, local_bands, 1))
        coupling = lax.psum(matmul(every_projector.T, vectors), "grid")
        exchange_part = matmul(every_projector, coupling)
        grid_field = vectors.reshape(grid_shape)
        applied = (-0.5 * laplacian(grid_field) + potential[..., None] * grid_field).reshape(
            -1, local_bands
        ) - exchange_part
        rayleigh = lax.psum(jnp.sum(vectors * applied, axis=0), "grid")
        residual = applied - rayleigh[None, :] * vectors
        squared = lax.psum(jnp.sum(residual * residual, axis=0), "grid")
        vectors = vectors - STEP_LENGTH * residual / jnp.sqrt(squared + NORM_EPS)[None, :]
        quotient_list.append(rayleigh)
        norm_list.append(jnp.sqrt(squared))
    return (vectors.reshape(grid_shape), jnp.stack(quotient_list), jnp.stack(norm_list))


def solution(mesh):
    return jax.shard_map(
        local,
        mesh=mesh,
        in_specs=(
            P("grid", None, None, "band"),
            P("grid", None, None, "band"),
            P("grid", None, None),
        ),
        out_specs=(P("grid", None, None, "band"), P(None, "band"), P(None, "band")),
        check_vma=False,
    )
```

profile of v0, /device:TPU:0, one launch (start us, length us, event | category | flops | bytes accessed | tf_op | source)
XLA Modules:
  0.0 1202.1 jit_solution(3516485684897773808)
XLA Ops:
  7.9 27.1 %all-gather.5.cloned.1.call-done = f32[4,16,16,512]{3,2,1,0:T(8,128)} async-done(((f32[4,16,16,128]{3,2,1,0:T(8,128)}), f32[4,16,16,512]{3,2,1,0:T(8,128)}) %all-gather.5.cloned.1.call-update) | async-done | bytes 2097168 | tf_op jit(solution)/shard_map/all_gather | solution.py:64
  43.0 77.3 %all-reduce.8.cloned.1.call-done = f32[512,512]{0,1:T(8,128)} async-done(((f32[512,512]{0,1:T(8,128)}), f32[512,512]{0,1:T(8,128)}) %all-reduce.8.cloned.1.call-update) | async-done | bytes 1048592 | tf_op jit(solution)/shard_map/psum | solution.py:67
  123.2 11.7 cholesky.374
  147.4 11.7 cholesky.393
  171.0 11.7 cholesky.414
  194.7 11.7 cholesky.431
  218.7 39.3 %custom-call.34 = f32[4,128,128]{1,2,0:T(8,128)S(1)} custom-call(f32[4,128,128]{2,1,0:T(8,128)S(1)} %get-tuple-element.25), custom_call_target="InvertDiagBlocksLowerTriangular" | custom-call | tf_op jit(solution)/shard_map/jit(_solve_triangular)/triangular_solve | solution.py:69
  296.4 58.0 %all-reduce.10.cloned.1.call-done = f32[512,128]{0,1:T(8,128)} async-done(((f32[512,128]{0,1:T(8,128)}), f32[512,128]{0,1:T(8,128)}) %all-reduce.10.cloned.1.call-update) | async-done | bytes 262160 | tf_op jit(solution)/shard_map/psum | solution.py:72
  357.9 19.6 %psum.86 = f32[128]{0:T(128)S(1)} all-reduce(f32[128]{0:T(128)S(1)} %get-tuple-element.195), channel_id=1, replica_groups=mesh['grid'=8,'band'=4] {'grid'}, use_global_device_ids=true, to_apply=%region_11.14 | all-reduce | flops 128 | bytes 1024 | tf_op jit(solution)/shard_map/psum | solution.py:78
  377.8 17.1 %psum.87 = f32[128]{0:T(128)S(1)} all-reduce(f32[128]{0:T(128)S(1)} %multiply_reduce_fusion.4), channel_id=1, replica_groups=mesh['grid'=8,'band'=4] {'grid'}, use_global_device_ids=true, to_apply=%region_13.16 | all-reduce | flops 128 | bytes 1024 | tf_op jit(solution)/shard_map/psum | solution.py:80
  398.0 21.6 %all-gather.9.cloned.1.call-done = f32[4,16,16,512]{3,2,1,0:T(8,128)} async-done(((f32[4,16,16,128]{3,2,1,0:T(8,128)}), f32[4,16,16,512]{3,2,1,0:T(8,128)}) %all-gather.9.cloned.1.call-update) | async-done | bytes 2097168 | tf_op jit(solution)/shard_map/all_gather | solution.py:64
  426.8 77.9 %all-reduce.12.cloned.1.call-done = f32[512,512]{0,1:T(8,128)} async-done(((f32[512,512]{0,1:T(8,128)}), f32[512,512]{0,1:T(8,128)}) %all-reduce.12.cloned.1.call-update) | async-done | bytes 1048592 | tf_op jit(solution)/shard_map/psum | solution.py:67
  509.8 11.7 cholesky.446
  534.0 11.7 cholesky.465
  559.6 11.7 cholesky.486
  584.6 11.7 cholesky.503
  602.6 11.8 while.7
  615.1 40.1 %custom-call.38 = f32[4,128,128]{1,2,0:T(8,128)S(1)} custom-call(f32[4,128,128]{2,1,0:T(8,128)} %copy-done.45), custom_call_target="InvertDiagBlocksLowerTriangular" | custom-call | tf_op jit(solution)/shard_map/jit(_solve_triangular)/triangular_solve | solution.py:69
  680.7 14.4 %collective-permute-done.2 = f32[4,16,16,128]{3,2,1,0:T(8,128)} collective-permute-done((f32[4,16,16,128]{3,2,1,0:T(8,128)S(1)}, f32[4,16,16,128]{3,2,1,0:T(8,128)}, u32[]{:S(2)}, u32[]{:S(2)}) %collective-permute-start.2) | collective-permute-done | bytes 524320 | tf_op jit(solution)/shard_map/ppermute | solution.py:24
  701.9 51.0 %all-reduce.14.cloned.1.call-done = f32[512,128]{0,1:T(8,128)} async-done(((f32[512,128]{0,1:T(8,128)}), f32[512,128]{0,1:T(8,128)}) %all-reduce.14.cloned.1.call-update) | async-done | bytes 262160 | tf_op jit(solution)/shard_map/psum | solution.py:72
  756.4 19.6 %psum.90 = f32[128]{0:T(128)S(1)} all-reduce(f32[128]{0:T(128)S(1)} %get-tuple-element.199), channel_id=1, replica_groups=mesh['grid'=8,'band'=4] {'grid'}, use_global_device_ids=true, to_apply=%region_17.20 | all-reduce | flops 128 | bytes 1024 | tf_op jit(solution)/shard_map/psum | solution.py:78
  776.2 17.1 %psum.91 = f32[128]{0:T(128)S(1)} all-reduce(f32[128]{0:T(128)S(1)} %multiply_reduce_fusion.2), channel_id=1, replica_groups=mesh['grid'=8,'band'=4] {'grid'}, use_global_device_ids=true, to_apply=%region_19.22 | all-reduce | flops 128 | bytes 1024 | tf_op jit(solution)/shard_map/psum | solution.py:80
  797.0 21.6 %all-gather.11.cloned.1.call-done = f32[4,16,16,512]{3,2,1,0:T(8,128)} async-done(((f32[4,16,16,128]{3,2,1,0:T(8,128)}), f32[4,16,16,512]{3,2,1,0:T(8,128)}) %all-gather.11.cloned.1.call-update) | async-done | bytes 2097168 | tf_op jit(solution)/shard_map/all_gather | solution.py:64
  825.5 78.3 %all-reduce.16.cloned.1.call-done = f32[512,512]{0,1:T(8,128)} async-done(((f32[512,512]{0,1:T(8,128)}), f32[512,512]{0,1:T(8,128)}) %all-reduce.16.cloned.1.call-update) | async-done | bytes 1048592 | tf_op jit(solution)/shard_map/psum | solution.py:67
  908.8 11.7 cholesky.518
  983.7 11.7 cholesky.575
  1001.9 11.8 while.8
  1014.4 40.1 %custom-call.42 = f32[4,128,128]{1,2,0:T(8,128)S(1)} custom-call(f32[4,128,128]{2,1,0:T(8,128)} %copy-done.44), custom_call_target="InvertDiagBlocksLowerTriangular" | custom-call | tf_op jit(solution)/shard_map/jit(_solve_triangular)/triangular_solve | solution.py:69
  1079.6 14.8 %collective-permute-done.4 = f32[4,16,16,128]{3,2,1,0:T(8,128)} collective-permute-done((f32[4,16,16,128]{3,2,1,0:T(8,128)S(1)}, f32[4,16,16,128]{3,2,1,0:T(8,128)}, u32[]{:S(2)}, u32[]{:S(2)}) %collective-permute-start.4) | collective-permute-done | bytes 524320 | tf_op jit(solution)/shard_map/ppermute | solution.py:24
  1101.2 51.0 %all-reduce.18.cloned.1.call-done = f32[512,128]{0,1:T(8,128)} async-done(((f32[512,128]{0,1:T(8,128)}), f32[512,128]{0,1:T(8,128)}) %all-reduce.18.cloned.1.call-update) | async-done | bytes 262160 | tf_op jit(solution)/shard_map/psum | solution.py:72
  1155.7 19.6 %psum.94 = f32[128]{0:T(128)S(1)} all-reduce(f32[128]{0:T(128)S(1)} %get-tuple-element.203), channel_id=1, replica_groups=mesh['grid'=8,'band'=4] {'grid'}, use_global_device_ids=true, to_apply=%region_23.26 | all-reduce | flops 128 | bytes 1024 | tf_op jit(solution)/shard_map/psum | solution.py:78
  1175.5 17.1 %psum.95 = f32[128]{0:T(128)S(1)} all-reduce(f32[128]{0:T(128)S(1)} %multiply_reduce_fusion), channel_id=1, replica_groups=mesh['grid'=8,'band'=4] {'grid'}, use_global_device_ids=true, to_apply=%region_25.28 | all-reduce | flops 128 | bytes 1024 | tf_op jit(solution)/shard_map/psum | solution.py:80
  (345 shorter events, 347.1 us)
Async XLA Ops:
  7.2 27.9 %all-gather.5.cloned.1.call-start = ((), (), s32[]{:S(2)}) async-start(), calls=%async_computation | async-start | bytes 2621440 | tf_op jit(solution)/shard_map/all_gather | solution.py:64
  7.9 112.4 %all-reduce.8.cloned.1.call-start = ((), (), s32[]{:S(2)}) async-start(), calls=%async_computation.1 | async-start | bytes 2097152 | tf_op jit(solution)/shard_map/psum | solution.py:67
  41.8 236.4 %all-gather.7.cloned.1.call-start = ((), (), s32[]{:S(2)}) async-start(), calls=%async_computation.2 | async-start | bytes 2621440 | tf_op jit(solution)/shard_map/all_gather | solution.py:57
  42.5 311.9 %all-reduce.10.cloned.1.call-start = ((), (), s32[]{:S(2)}) async-start(), calls=%async_computation.3 | async-start | bytes 524288 | tf_op jit(solution)/shard_map/psum | solution.py:72
  43.0 217.1 %copy-start.4 = (f32[512,512]{1,0:T(8,128)}, f32[512,512]{1,0:T(8,128)S(1)}, u32[]{:S(2)}) copy-start(f32[512,512]{1,0:T(8,128)S(1)} %fusion.6) | copy-start | bytes 3145732
  263.7 24.9 %collective-permute-start = (f32[4,16,16,128]{3,2,1,0:T(8,128)S(1)}, f32[4,16,16,128]{3,2,1,0:T(8,128)S(1)}, u32[]{:S(2)}, u32[]{:S(2)}) collective-permute-start(f32[4,16,16,128]{3,2,1,0:T(8,128)S(1)} %bitcast.253), channel_id=1, source_target_pairs={{4,0},{8,4},{12,8},{16,12},{20,16},{24,20},{28,24},{0,28},{5,1},{9... | collective-permute-start | bytes 1572872 | tf_op jit(solution)/shard_map/ppermute | solution.py:24
  266.7 21.9 %collective-permute-start.1 = (f32[4,16,16,128]{3,2,1,0:T(8,128)S(1)}, f32[4,16,16,128]{3,2,1,0:T(8,128)S(1)}, u32[]{:S(2)}, u32[]{:S(2)}) collective-permute-start(f32[4,16,16,128]{3,2,1,0:T(8,128)S(1)} %bitcast.254), channel_id=1, source_target_pairs={{0,4},{4,8},{8,12},{12,16},{16,20},{20,24},{24,28},{28,0},{1,5},{5... | collective-permute-start | bytes 1572872 | tf_op jit(solution)/shard_map/ppermute | solution.py:21
  281.8 137.8 %all-gather.9.cloned.1.call-start = ((), (), s32[]{:S(2)}) async-start(), calls=%async_computation.4 | async-start | bytes 2621440 | tf_op jit(solution)/shard_map/all_gather | solution.py:64
  289.6 64.8 %copy-start = (f32[4,16,16,512]{3,2,1,0:T(8,128)S(1)}, f32[4,16,16,512]{3,2,1,0:T(8,128)}, u32[]{:S(2)}) copy-start(f32[4,16,16,512]{3,2,1,0:T(8,128)} %all-gather.7.cloned.1.call-done) | copy-start | bytes 6291460
  398.0 106.8 %all-reduce.12.cloned.1.call-start = ((), (), s32[]{:S(2)}) async-start(), calls=%async_computation.5 | async-start | bytes 2097152 | tf_op jit(solution)/shard_map/psum | solution.py:67
  426.3 326.6 %all-reduce.14.cloned.1.call-start = ((), (), s32[]{:S(2)}) async-start(), calls=%async_computation.6 | async-start | bytes 524288 | tf_op jit(solution)/shard_map/psum | solution.py:72
  559.6 95.7 %copy-start.5 = (f32[512,512]{1,0:T(8,128)S(1)}, f32[512,512]{1,0:T(8,128)}, u32[]{:S(2)}) copy-start(f32[512,512]{1,0:T(8,128)} %copy-done.4) | copy-start | bytes 3145732
  669.1 26.0 %collective-permute-start.2 = (f32[4,16,16,128]{3,2,1,0:T(8,128)S(1)}, f32[4,16,16,128]{3,2,1,0:T(8,128)}, u32[]{:S(2)}, u32[]{:S(2)}) collective-permute-start(f32[4,16,16,128]{3,2,1,0:T(8,128)S(1)} %bitcast.221), channel_id=1, source_target_pairs={{4,0},{8,4},{12,8},{16,12},{20,16},{24,20},{28,24},{0,28},{5,1},{9... | collective-permute-start | bytes 1572872 | tf_op jit(solution)/shard_map/ppermute | solution.py:24
  672.0 23.1 %collective-permute-start.3 = (f32[4,16,16,128]{3,2,1,0:T(8,128)S(1)}, f32[4,16,16,128]{3,2,1,0:T(8,128)}, u32[]{:S(2)}, u32[]{:S(2)}) collective-permute-start(f32[4,16,16,128]{3,2,1,0:T(8,128)S(1)} %bitcast.222), channel_id=1, source_target_pairs={{0,4},{4,8},{8,12},{12,16},{16,20},{20,24},{24,28},{28,0},{1,5},{5... | collective-permute-start | bytes 1572872 | tf_op jit(solution)/shard_map/ppermute | solution.py:21
  680.0 138.6 %all-gather.11.cloned.1.call-start = ((), (), s32[]{:S(2)}) async-start(), calls=%async_computation.7 | async-start | bytes 2621440 | tf_op jit(solution)/shard_map/all_gather | solution.py:64
  680.4 14.7 %copy-start.15 = (f32[4,16,15,128]{3,2,1,0:T(8,128)S(1)}, f32[4,16,15,128]{3,2,1,0:T(8,128)}, u32[]{:S(2)}) copy-start(f32[4,16,15,128]{3,2,1,0:T(8,128)} %get-tuple-element.111) | copy-start | bytes 1474564
  680.5 14.7 %copy-start.16 = (f32[4,16,15,128]{3,2,1,0:T(8,128)S(1)}, f32[4,16,15,128]{3,2,1,0:T(8,128)}, u32[]{:S(2)}) copy-start(f32[4,16,15,128]{3,2,1,0:T(8,128)} %get-tuple-element.112) | copy-start | bytes 1474564
  796.9 106.8 %all-reduce.16.cloned.1.call-start = ((), (), s32[]{:S(2)}) async-start(), calls=%async_computation.8 | async-start | bytes 2097152 | tf_op jit(solution)/shard_map/psum | solution.py:67
  825.3 326.9 %all-reduce.18.cloned.1.call-start = ((), (), s32[]{:S(2)}) async-start(), calls=%async_computation.9 | async-start | bytes 524288 | tf_op jit(solution)/shard_map/psum | solution.py:72
  958.7 95.8 %copy-start.6 = (f32[512,512]{1,0:T(8,128)S(1)}, f32[512,512]{1,0:T(8,128)}, u32[]{:S(2)}) copy-start(f32[512,512]{1,0:T(8,128)} %copy-done.4) | copy-start | bytes 3145732
  1068.4 26.0 %collective-permute-start.4 = (f32[4,16,16,128]{3,2,1,0:T(8,128)S(1)}, f32[4,16,16,128]{3,2,1,0:T(8,128)}, u32[]{:S(2)}, u32[]{:S(2)}) collective-permute-start(f32[4,16,16,128]{3,2,1,0:T(8,128)S(1)} %bitcast.240), channel_id=1, source_target_pairs={{4,0},{8,4},{12,8},{16,12},{20,16},{24,20},{28,24},{0,28},{5,1},{9... | collective-permute-start | bytes 1572872 | tf_op jit(solution)/shard_map/ppermute | solution.py:24
  1071.3 23.1 %collective-permute-start.5 = (f32[4,16,16,128]{3,2,1,0:T(8,128)S(1)}, f32[4,16,16,128]{3,2,1,0:T(8,128)}, u32[]{:S(2)}, u32[]{:S(2)}) collective-permute-start(f32[4,16,16,128]{3,2,1,0:T(8,128)S(1)} %bitcast.241), channel_id=1, source_target_pairs={{0,4},{4,8},{8,12},{12,16},{16,20},{20,24},{24,28},{28,0},{1,5},{5... | collective-permute-start | bytes 1572872 | tf_op jit(solution)/shard_map/ppermute | solution.py:21
  1079.4 15.0 %copy-start.21 = (f32[4,16,15,128]{3,2,1,0:T(8,128)S(1)}, f32[4,16,15,128]{3,2,1,0:T(8,128)}, u32[]{:S(2)}) copy-start(f32[4,16,15,128]{3,2,1,0:T(8,128)} %get-tuple-element.79) | copy-start | bytes 1474564
  1079.4 15.0 %copy-start.22 = (f32[4,16,15,128]{3,2,1,0:T(8,128)S(1)}, f32[4,16,15,128]{3,2,1,0:T(8,128)}, u32[]{:S(2)}) copy-start(f32[4,16,15,128]{3,2,1,0:T(8,128)} %get-tuple-element.80) | copy-start | bytes 1474564
  1079.4 15.0 %copy-start.23 = (f32[4,16,14,128]{3,2,1,0:T(8,128)S(1)}, f32[4,16,14,128]{3,2,1,0:T(8,128)}, u32[]{:S(2)}) copy-start(f32[4,16,14,128]{3,2,1,0:T(8,128)} %get-tuple-element.83) | copy-start | bytes 1376260
  1079.4 15.0 %copy-start.24 = (f32[4,16,14,128]{3,2,1,0:T(8,128)S(1)}, f32[4,16,14,128]{3,2,1,0:T(8,128)}, u32[]{:S(2)}) copy-start(f32[4,16,14,128]{3,2,1,0:T(8,128)} %get-tuple-element.84) | copy-start | bytes 1376260
  1079.4 15.0 %copy-start.25 = (f32[4,16,13,128]{3,2,1,0:T(8,128)S(1)}, f32[4,16,13,128]{3,2,1,0:T(8,128)}, u32[]{:S(2)}) copy-start(f32[4,16,13,128]{3,2,1,0:T(8,128)} %get-tuple-element.87) | copy-start | bytes 1277956
  1079.4 15.0 %copy-start.26 = (f32[4,16,13,128]{3,2,1,0:T(8,128)S(1)}, f32[4,16,13,128]{3,2,1,0:T(8,128)}, u32[]{:S(2)}) copy-start(f32[4,16,13,128]{3,2,1,0:T(8,128)} %get-tuple-element.88) | copy-start | bytes 1277956
  1079.4 15.0 %copy-start.35 = (f32[4,14,16,128]{3,2,1,0:T(8,128)S(1)}, f32[4,14,16,128]{3,2,1,0:T(8,128)}, u32[]{:S(2)}) copy-start(f32[4,14,16,128]{3,2,1,0:T(8,128)} %get-tuple-element.67) | copy-start | bytes 1376260
  1079.4 15.0 %copy-start.36 = (f32[4,14,16,128]{3,2,1,0:T(8,128)S(1)}, f32[4,14,16,128]{3,2,1,0:T(8,128)}, u32[]{:S(2)}) copy-start(f32[4,14,16,128]{3,2,1,0:T(8,128)} %get-tuple-element.68) | copy-start | bytes 1376260
  1079.5 15.0 %copy-start.43 = (f32[4,16,16]{2,1,0:T(8,128)S(1)}, f32[4,16,16]{2,1,0:T(8,128)}, u32[]{:S(2)}) copy-start(f32[4,16,16]{2,1,0:T(8,128)} %param.8) | copy-start | bytes 12292
  1155.7 38.2 %copy-start.46 = (f32[1,128]{1,0:T(1,128)S(1)}, f32[1,128]{1,0:T(1,128)}, u32[]{:S(2)}) copy-start(f32[1,128]{1,0:T(1,128)} %get-tuple-element.189) | copy-start | bytes 1540
  (31 other events, 195.8 us)
Sparse Core Ops, SparseCore 0:
  9.5 25.5 all-gather.4
  41.9 78.3 all-reduce.7
  121.8 22.4 all-gather.6
  282.0 72.4 all-reduce.9
  398.1 21.4 all-gather.8
  426.4 78.2 all-reduce.11
  680.1 72.7 all-reduce.13
  797.0 21.4 all-gather.10
  825.4 78.3 all-reduce.15
  1079.5 72.6 all-reduce.17
where the time goes:
time: 1210 us; the launch traced here: 1200 us
  waiting for transfers between devices  501 us (41%)
  other arithmetic  387 us (32%)
  blocking collectives  110 us (9%)
  local copies, waits for them, and re-layouts  93.1 us (8%)
  matrix products  77.4 us (6%)
  between operations  22.9 us (2%)
    another operation x44, other arithmetic, local(): factor = jnp.linalg.cholesky(margin)  240 us
    psum x3, waiting for transfers between devices, local(): margin = lax.psum(matmul(gathered.T, gathered), 'grid')  233 us
    psum x3, waiting for transfers between devices, local(): coupling = lax.psum(matmul(every_projector.T, vectors), 'grid')  160 us
    another operation x7, other arithmetic, local(): jax.scipy.linalg.solve_triangular(factor, identity_matrix, lower=True)  125 us
    all_gather x3, waiting for transfers between devices, local(): lax.all_gather(vectors.reshape(grid_shape), 'band', axis=3, tiled=True)  70.3 us
    psum x3, blocking collectives, local(): rayleigh = lax.psum(jnp.sum(vectors * applied, axis=0), 'grid')  58.9 us
    psum x3, blocking collectives, local(): squared = lax.psum(jnp.sum(residual * residual, axis=0), 'grid')  51.4 us
    dot_general x12, matrix products, matmul(): jnp.dot(left, right, precision=HIGHEST, preferred_element_type=jnp.float32)  44.3 us
  transfers between devices with their start and end apart: 16, of which 12 were waited for; matrix products, arithmetic and copies ran while one was open for 16% of the time, Pallas kernels for 0%

commit v1 on v0

--- a/solution.py
+++ b/solution.py
@@ -1,6 +1,10 @@
+import functools
+
 import jax
 import jax.numpy as jnp
 from jax import lax
+from jax.experimental import pallas as pl
+from jax.experimental.pallas import tpu as pltpu
 from jax.sharding import PartitionSpec as P
 
 ITERS = 3
@@ -10,6 +14,8 @@
 STEP_LENGTH = 0.25
 NORM_EPS = 1e-06
 HIGHEST = lax.Precision.HIGHEST
+MESH = pl.DeviceIdType.MESH
+VMEM = pl.BlockSpec(memory_space=pltpu.VMEM)
 
 
 def with_halo(block, sides, width):
@@ -48,40 +54,315 @@
     return result
 
 
+def dot_in_kernel(left, right, contract):
+    return lax.dot_general(
+        left, right, (contract, ((), ())), precision=HIGHEST, preferred_element_type=jnp.float32
+    )
+
+
+def block_inverse_factor(block):
+    size = block.shape[0]
+    groups = [block[8 * g : 8 * g + 8, :] for g in range(size // 8)]
+    lane = lax.broadcasted_iota(jnp.int32, (8, size), 1)
+    sublane = lax.broadcasted_iota(jnp.int32, (8, size), 0)
+    finished = []
+    for g in range(size // 8):
+        result = jnp.zeros((8, size), jnp.float32)
+        for s in range(8):
+            j = 8 * g + s
+            row = jnp.broadcast_to(groups[g][s : s + 1, :], (8, size))
+            pivot = jnp.broadcast_to(row[:, j : j + 1], (8, size))
+            at_pivot = lane == j
+            row = jnp.where(at_pivot, 1.0, row)
+            scaled = row * (1.0 / pivot)
+            result = jnp.where(
+                (sublane == s) & (lane <= j), row * (1.0 / jnp.sqrt(pivot)), result
+            )
+            for i in range(g, size // 8):
+                column = jnp.broadcast_to(groups[i][:, j : j + 1], (8, size))
+                groups[i] = jnp.where(at_pivot, 0.0, groups[i]) - column * scaled if i > g else (
+                    jnp.where(
+                        sublane > s,
+                        jnp.where(at_pivot, 0.0, groups[i]) - column * scaled,
+                        groups[i],
+                    )
+                )
+        finished.append(result)
+    return jnp.concatenate(finished, axis=0)
+
+
+def inverse_factor_kernel(size, block, margin_ref, out_ref, work, panel):
+    work[...] = margin_ref[...]
+    count = size // block
+
+    @pl.loop(0, count)
+    def _(k):
+        here = pl.ds(pl.multiple_of(k * block, block), block)
+        inverse = block_inverse_factor(work[here, here])
+        rows = dot_in_kernel(inverse, work[here, :], ((1,), (0,)))
+        panel[...] = rows
+        work[here, :] = rows
+        work[here, here] = inverse
+
+        @pl.loop(k + 1, count)
+        def _(i):
+            there = pl.ds(pl.multiple_of(i * block, block), block)
+            work[there, here] = jnp.zeros((block, block), jnp.float32)
+            work[there, :] = work[there, :] - dot_in_kernel(
+                panel[:, there], work[here, :], ((0,), (0,))
+            )
+
+    for r in range(count):
+        rows = pl.ds(r * block, block)
+        out_ref[rows, :] = jnp.zeros((block, size), jnp.float32)
+        out_ref[rows, : (r + 1) * block] = work[rows, : (r + 1) * block]
+
+
+def inverse_factor(margin, block):
+    size = margin.shape[0]
+    return pl.pallas_call(
+        functools.partial(inverse_factor_kernel, size, block),
+        out_shape=jax.ShapeDtypeStruct((size, size), jnp.float32),
+        in_specs=[VMEM],
+        out_specs=VMEM,
+        scratch_shapes=[
+            pltpu.VMEM((size, size), jnp.float32),
+            pltpu.VMEM((block, size), jnp.float32),
+        ],
+    )(margin)
+
+
+def greet(axis, count, me):
+    barrier = pltpu.get_barrier_semaphore()
+    for k in range(1, count):
+        pl.semaphore_signal(
+            barrier, inc=1, device_id={axis: lax.rem(me + k, count)}, device_id_type=MESH
+        )
+    pl.semaphore_wait(barrier, count - 1)
+
+
+def remote(axis, peer, source, target, send_sem, recv_sem):
+    return pltpu.make_async_remote_copy(
+        src_ref=source,
+        dst_ref=target,
+        send_sem=send_sem,
+        recv_sem=recv_sem,
+        device_id={axis: peer},
+        device_id_type=MESH,
+    )
+
+
+def grid_sum_kernel(count, x_ref, out_ref, parts, mine, total, s1, r1, s2, r2):
+    me = lax.axis_index("grid")
+    chunk = x_ref.shape[0] // count
+    greet("grid", count, me)
+    copies = []
+    for k in range(1, count):
+        peer = lax.rem(me + k, count)
+        copy = remote(
+            "grid",
+            peer,
+            x_ref.at[pl.ds(pl.multiple_of(peer * chunk, chunk), chunk), :],
+            parts.at[k - 1],
+            s1.at[k - 1],
+            r1.at[k - 1],
+        )
+        copy.start()
+        copies.append(copy)
+    own = pl.ds(pl.multiple_of(me * chunk, chunk), chunk)
+    mine[...] = x_ref[own, :]
+    for k in range(1, count):
+        copies[k - 1].wait_recv()
+        mine[...] += parts[k - 1]
+    total[me] = mine[...]
+    back = []
+    for k in range(1, count):
+        peer = lax.rem(me + k, count)
+        copy = remote("grid", peer, mine, total.at[me], s2.at[k - 1], r2.at[k - 1])
+        copy.start()
+        back.append(copy)
+    for k in range(1, count):
+        copies[k - 1].wait_send()
+        back[k - 1].wait()
+    for c in range(count):
+        out_ref[c * chunk : (c + 1) * chunk, :] = total[c]
+
+
+def grid_sum(x):
+    count = lax.axis_size("grid")
+    rows, columns = x.shape
+    chunk = rows // count
+    sems = pltpu.SemaphoreType.DMA((count - 1,))
+    return pl.pallas_call(
+        functools.partial(grid_sum_kernel, count),
+        out_shape=jax.ShapeDtypeStruct(x.shape, jnp.float32),
+        in_specs=[VMEM],
+        out_specs=VMEM,
+        scratch_shapes=[
+            pltpu.VMEM((count - 1, chunk, columns), jnp.float32),
+            pltpu.VMEM((chunk, columns), jnp.float32),
+            pltpu.VMEM((count, chunk, columns), jnp.float32),
+            sems,
+            sems,
+            sems,
+            sems,
+        ],
+        compiler_params=pltpu.CompilerParams(collective_id=1, has_side_effects=True),
+        cost_estimate=pl.CostEstimate(flops=10**6, bytes_accessed=4 * 10**7, transcendentals=0),
+    )(x)
+
+
+def band_gather_kernel(count, x_ref, out_ref, held, send, recv):
+    me = lax.axis_index("band")
+    width = x_ref.shape[1]
+    if count == 4:
+        half, side = lax.div(me, 2), lax.rem(me, 2)
+        partner = half * 2 + 1 - side
+        across = (1 - half) * 2 + side
+        barrier = pltpu.get_barrier_semaphore()
+        for peer in (partner, across):
+            pl.semaphore_signal(barrier, inc=1, device_id={"band": peer}, device_id_type=MESH)
+        pl.semaphore_wait(barrier, 2)
+        far = remote("band", across, x_ref, held.at[0], send.at[0], recv.at[0])
+        far.start()
+        near = remote("band", partner, x_ref, held.at[1], send.at[1], recv.at[1])
+        near.start()
+        out_ref[:, pl.ds(pl.multiple_of(me * width, width), width)] = x_ref[...]
+        far.wait_recv()
+        relay = remote("band", partner, held.at[0], held.at[2], send.at[2], recv.at[2])
+        relay.start()
+        near.wait_recv()
+        out_ref[:, pl.ds(pl.multiple_of(partner * width, width), width)] = held[1]
+        out_ref[:, pl.ds(pl.multiple_of(across * width, width), width)] = held[0]
+        relay.wait_recv()
+        opposite = (1 - half) * 2 + 1 - side
+        out_ref[:, pl.ds(pl.multiple_of(opposite * width, width), width)] = held[2]
+        far.wait_send()
+        near.wait_send()
+        relay.wait_send()
+    else:
+        greet("band", count, me)
+        copies = []
+        for k in range(1, count):
+            peer = lax.rem(me + k, count)
+            copy = remote("band", peer, x_ref, held.at[k - 1], send.at[k - 1], recv.at[k - 1])
+            copy.start()
+            copies.append(copy)
+        out_ref[:, pl.ds(pl.multiple_of(me * width, width), width)] = x_ref[...]
+        for k in range(1, count):
+            copies[k - 1].wait()
+            source = lax.rem(me + count - k, count)
+            out_ref[:, pl.ds(pl.multiple_of(source * width, width), width)] = held[k - 1]
+
+
+def band_gather(x, collective):
+    count = lax.axis_size("band")
+    rows, columns = x.shape
+    return pl.pallas_call(
+        functools.partial(band_gather_kernel, count),
+        out_shape=jax.ShapeDtypeStruct((rows, columns * count), jnp.float32),
+        in_specs=[VMEM],
+        out_specs=VMEM,
+        scratch_shapes=[
+            pltpu.VMEM((count - 1, rows, columns), jnp.float32),
+            pltpu.SemaphoreType.DMA((count - 1,)),
+            pltpu.SemaphoreType.DMA((count - 1,)),
+        ],
+        compiler_params=pltpu.CompilerParams(collective_id=collective, has_side_effects=True),
+        cost_estimate=pl.CostEstimate(flops=10**6, bytes_accessed=4 * 10**7, transcendentals=0),
+    )(x)
+
+
+def update_kernel(
+    count, v_ref, w_ref, out_ref, quotient_ref, norm_ref, part1, part2, all1, all2, s1, r1, s2, r2
+):
+    me = lax.axis_index("grid")
+    cells, bands = v_ref.shape
+    greet("grid", count, me)
+
+    def exchange(value, part, everyone, send, recv):
+        part[...] = value
+        everyone[me] = value
+        copies = []
+        for k in range(1, count):
+            peer = lax.rem(me + k, count)
+            copy = remote("grid", peer, part, everyone.at[me], send.at[k - 1], recv.at[k - 1])
+            copy.start()
+            copies.append(copy)
+        for copy in copies:
+            copy.wait()
+        total = everyone[0]
+        for c in range(1, count):
+            total = total + everyone[c]
+        return jnp.sum(total, axis=0, keepdims=True)
+
+    products = v_ref[...] * w_ref[...]
+    quotient = exchange(
+        jnp.sum(products.reshape(cells // 8, 8, bands), axis=0), part1, all1, s1, r1
+    )
+    quotient_ref[...] = quotient
+    residual = w_ref[...] - quotient * v_ref[...]
+    squared = exchange(
+        jnp.sum((residual * residual).reshape(cells // 8, 8, bands), axis=0), part2, all2, s2, r2
+    )
+    norm_ref[...] = jnp.sqrt(squared)
+    factor = STEP_LENGTH / jnp.sqrt(squared + NORM_EPS)
+    out_ref[...] = v_ref[...] - (w_ref[...] - quotient * v_ref[...]) * factor
+
+
+def update(vectors, applied):
+    count = lax.axis_size("grid")
+    bands = vectors.shape[1]
+    sems = pltpu.SemaphoreType.DMA((count - 1,))
+    small = pltpu.VMEM((8, bands), jnp.float32)
+    everyone = pltpu.VMEM((count, 8, bands), jnp.float32)
+    line = jax.ShapeDtypeStruct((1, bands), jnp.float32)
+    return pl.pallas_call(
+        functools.partial(update_kernel, count),
+        out_shape=(jax.ShapeDtypeStruct(vectors.shape, jnp.float32), line, line),
+        in_specs=[VMEM, VMEM],
+        out_specs=(VMEM, VMEM, VMEM),
+        scratch_shapes=[small, small, everyone, everyone, sems, sems, sems, sems],
+        compiler_params=pltpu.CompilerParams(collective_id=4, has_side_effects=True),
+    )(vectors, applied)
+
+
 def local(orbitals, projectors, potential):
     grid_shape = orbitals.shape
     local_bands = orbitals.shape[3]
-    total_bands = local_bands * lax.axis_size("band")
     first_band = lax.axis_index("band") * local_bands
     vectors = orbitals.reshape(-1, local_bands)
     every_projector = lax.all_gather(projectors, "band", axis=3, tiled=True).reshape(
         -1, projectors.shape[3] * lax.axis_size("band")
     )
-    identity_matrix = jnp.eye(total_bands, dtype=jnp.float32)
     quotient_list = []
     norm_list = []
     for iteration in range(ITERS):
-        gathered = lax.all_gather(vectors.reshape(grid_shape), "band", axis=3, tiled=True).reshape(
-            -1, total_bands
-        )
-        margin = lax.psum(matmul(gathered.T, gathered), "grid")
-        factor = jnp.linalg.cholesky(margin)
-        inverse = jax.scipy.linalg.solve_triangular(factor, identity_matrix, lower=True)
-        transform = inverse.T
-        vectors = matmul(gathered, lax.dynamic_slice_in_dim(transform, first_band, local_bands, 1))
-        coupling = lax.psum(matmul(every_projector.T, vectors), "grid")
+        gathered = band_gather(vectors, 2)
+        margin = band_gather(grid_sum(matmul(gathered.T, vectors)), 3)
+        inverse = inverse_factor(margin, local_bands)
+        rows = lax.dynamic_slice_in_dim(inverse, first_band, local_bands, 0)
+        vectors = lax.dot_general(
+            gathered,
+            rows,
+            (((1,), (1,)), ((), ())),
+            precision=HIGHEST,
+            preferred_element_type=jnp.float32,
+        )
+        coupling = grid_sum(matmul(every_projector.T, vectors))
         exchange_part = matmul(every_projector, coupling)
         grid_field = vectors.reshape(grid_shape)
         applied = (-0.5 * laplacian(grid_field) + potential[..., None] * grid_field).reshape(
             -1, local_bands
         ) - exchange_part
-        rayleigh = lax.psum(jnp.sum(vectors * applied, axis=0), "grid")
-        residual = applied - rayleigh[None, :] * vectors
-        squared = lax.psum(jnp.sum(residual * residual, axis=0), "grid")
-        vectors = vectors - STEP_LENGTH * residual / jnp.sqrt(squared + NORM_EPS)[None, :]
+        vectors, rayleigh, norm = update(vectors, applied)
         quotient_list.append(rayleigh)
-        norm_list.append(jnp.sqrt(squared))
-    return (vectors.reshape(grid_shape), jnp.stack(quotient_list), jnp.stack(norm_list))
+        norm_list.append(norm)
+    return (
+        vectors.reshape(grid_shape),
+        jnp.concatenate(quotient_list, axis=0),
+        jnp.concatenate(norm_list, axis=0),
+    )
 
 
 def solution(mesh):

time: 1210 us -> 629 us (0.52)
  waiting for transfers between devices: 501 us -> 19.4 us
  Pallas kernels: 0 us -> 481 us
  other arithmetic: 387 us -> 12.6 us
  blocking collectives: 110 us -> 0 us
  local copies, waits for them, and re-layouts: 93.1 us -> 30.9 us
  matrix products: 77.4 us -> 50.1 us
    pallas_call x0 -> x18, Pallas kernels: none -> 481 us  [the longest x3 226 us: inverse_factor(): pl.pallas_call(functools.partial(inverse_factor_kernel, size, block), out...]
    psum x6 -> x0, waiting for transfers between devices: 394 us -> none  [the longest x3 233 us: local(): margin = lax.psum(matmul(gathered.T, gathered), 'grid')]
    another operation x56 -> x0, other arithmetic: 367 us -> none  [the longest x44 240 us: local(): factor = jnp.linalg.cholesky(margin)]
    psum x6 -> x0, blocking collectives: 110 us -> none  [the longest x3 58.9 us: local(): rayleigh = lax.psum(jnp.sum(vectors * applied, axis=0), 'grid')]
    all_gather x3 -> x0, waiting for transfers between devices: 70.3 us -> none  [local(): lax.all_gather(vectors.reshape(grid_shape), 'band', axis=3, tiled=True)]
    another operation x39 -> x0, matrix products: 33.1 us -> none  [the longest x18 18 us: local(): factor = jnp.linalg.cholesky(margin)]
    another operation x52 -> x0, local copies, waits for them, and re-layouts: 31.9 us -> none  [the longest x40 31.5 us: local(): jax.scipy.linalg.solve_triangular(factor, identity_matrix, lower=True)]
    ppermute x3, waiting for transfers between devices: 35.4 us -> 19.4 us  [with_halo(): lax.ppermute(lax.slice_in_dim(block, 0, width, axis=dim), axis, backward)]
  transfers between devices with their start and end apart: 16 -> 7, of which waited for: 12 -> 1; matrix products, arithmetic and copies ran while one was open for 16% -> 4% of each run, Pallas kernels for 0% -> 8%
where the time goes in v1:
time: 629 us; the launch traced here: 620 us
  Pallas kernels  481 us (76%)
  matrix products  50.1 us (8%)
  local copies, waits for them, and re-layouts  30.9 us (5%)
  waiting for transfers between devices  19.4 us (3%)
  between operations  15.2 us (2%)
  other arithmetic  12.6 us (2%)
  starting transfers between devices  11.4 us (2%)
    pallas_call x3, Pallas kernels, inverse_factor(): pl.pallas_call(functools.partial(inverse_factor_kernel, size, block), out...  226 us
    pallas_call x6, Pallas kernels, grid_sum(): pl.pallas_call(functools.partial(grid_sum_kernel, count), out_shape=jax.S...  121 us
    pallas_call x6, Pallas kernels, band_gather(): pl.pallas_call(functools.partial(band_gather_kernel, count), out_shape=ja...  88.1 us
    pallas_call x3, Pallas kernels, update(): pl.pallas_call(functools.partial(update_kernel, count), out_shape=(jax.Sh...  45.8 us
    dot_general x9, matrix products, matmul(): jnp.dot(left, right, precision=HIGHEST, preferred_element_type=jnp.float32)  40.1 us
    slice x48, local copies, waits for them, and re-layouts, laplacian(): jnp.roll(grid_field, distance, dimension)  24.3 us
    ppermute x3, waiting for transfers between devices, with_halo(): lax.ppermute(lax.slice_in_dim(block, 0, width, axis=dim), axis, backward)  19.4 us
  transfers between devices with their start and end apart: 7, of which 1 were waited for; matrix products, arithmetic and copies ran while one was open for 4% of the time, Pallas kernels for 8%

profile of v1, /device:TPU:0, one launch (start us, length us, event | category | flops | bytes accessed | tf_op | source)
XLA Modules:
  0.0 620.2 jit_solution(10198517759789106809)
XLA Ops:
  7.2 19.5 %shard_map.58 = f32[1024,512]{1,0:T(8,128)} custom-call(f32[1024,128]{1,0:T(8,128)} %bitcast.114), custom_call_target="tpu_custom_call" | custom-call | flops 1000000 | bytes 40000000 | tf_op jit(solution)/shard_map/pallas_call | solution.py:261
  26.8 5.7 fusion.150.x_ref
  32.5 19.5 %shard_map.59.x_ref = f32[512,128]{1,0:T(8,128)} custom-call(f32[512,128]{1,0:T(8,128)} %fusion.150.x_ref), custom_call_target="tpu_custom_call" | custom-call | flops 1000000 | bytes 40000000 | tf_op jit(solution)/shard_map/pallas_call | solution.py:196
  52.0 11.2 %shard_map.60.margin_ref = f32[512,512]{1,0:T(8,128)} custom-call(f32[512,128]{1,0:T(8,128)} %shard_map.59.x_ref), custom_call_target="tpu_custom_call" | custom-call | flops 1000000 | bytes 40000000 | tf_op jit(solution)/shard_map/pallas_call | solution.py:261
  63.2 75.0 %shard_map.61 = f32[512,512]{1,0:T(8,128)} custom-call(f32[512,512]{1,0:T(8,128)} %shard_map.60.margin_ref), custom_call_target="tpu_custom_call" | custom-call | tf_op jit(solution)/shard_map/pallas_call | solution.py:123
  141.7 4.8 collective-permute-start
  147.9 19.3 %collective-permute-done = f32[4,16,16,128]{3,2,1,0:T(8,128)S(1)} collective-permute-done((f32[4,16,16,128]{3,2,1,0:T(8,128)S(1)}, f32[4,16,16,128]{3,2,1,0:T(8,128)S(1)}, u32[]{:S(2)}, u32[]{:S(2)}) %collective-permute-start) | collective-permute-done | bytes 524320 | tf_op jit(solution)/shard_map/ppermute | solution.py:30
  168.0 3.5 multiply_add_fusion.2
  171.6 5.9 convolution_bitcast_fusion.5.x_ref
  177.5 18.7 %shard_map.62 = f32[512,128]{1,0:T(8,128)} custom-call(f32[512,128]{1,0:T(8,128)} %convolution_bitcast_fusion.5.x_ref), custom_call_target="tpu_custom_call" | custom-call | flops 1000000 | bytes 40000000 | tf_op jit(solution)/shard_map/pallas_call | solution.py:196
  196.2 3.6 fusion.w_ref
  199.8 15.7 %shard_map.63 = (f32[1024,128]{1,0:T(8,128)}, f32[1,128]{1,0:T(1,128)}, f32[1,128]{1,0:T(1,128)}) custom-call(f32[1024,128]{1,0:T(8,128)} %bitcast.107, f32[1024,128]{1,0:T(8,128)} %fusion.w_ref), custom_call_target="tpu_custom_call" | custom-call | tf_op jit(solution)/shard_map/pallas_call | solution.py:320
  215.4 17.5 %shard_map.64 = f32[1024,512]{1,0:T(8,128)} custom-call(f32[1024,128]{1,0:T(8,128)} %get-tuple-element.12.x_ref), custom_call_target="tpu_custom_call" | custom-call | flops 1000000 | bytes 40000000 | tf_op jit(solution)/shard_map/pallas_call | solution.py:261
  233.0 5.7 fusion.151.x_ref
  238.7 17.2 %shard_map.65.x_ref = f32[512,128]{1,0:T(8,128)} custom-call(f32[512,128]{1,0:T(8,128)} %fusion.151.x_ref), custom_call_target="tpu_custom_call" | custom-call | flops 1000000 | bytes 40000000 | tf_op jit(solution)/shard_map/pallas_call | solution.py:196
  255.9 11.2 %shard_map.66.margin_ref = f32[512,512]{1,0:T(8,128)} custom-call(f32[512,128]{1,0:T(8,128)} %shard_map.65.x_ref), custom_call_target="tpu_custom_call" | custom-call | flops 1000000 | bytes 40000000 | tf_op jit(solution)/shard_map/pallas_call | solution.py:261
  267.1 75.2 %shard_map.67 = f32[512,512]{1,0:T(8,128)} custom-call(f32[512,512]{1,0:T(8,128)} %shard_map.66.margin_ref), custom_call_target="tpu_custom_call" | custom-call | tf_op jit(solution)/shard_map/pallas_call | solution.py:123
  342.3 3.4 fusion.95.v_ref
  360.4 4.1 convolution_bitcast_fusion.4.x_ref
  364.5 24.1 %shard_map.68 = f32[512,128]{1,0:T(8,128)} custom-call(f32[512,128]{1,0:T(8,128)} %convolution_bitcast_fusion.4.x_ref), custom_call_target="tpu_custom_call" | custom-call | flops 1000000 | bytes 40000000 | tf_op jit(solution)/shard_map/pallas_call | solution.py:196
  390.8 4.0 multiply_add_fusion.1
  397.4 15.1 %shard_map.69 = (f32[1024,128]{1,0:T(8,128)}, f32[1,128]{1,0:T(1,128)}, f32[1,128]{1,0:T(1,128)}) custom-call(f32[1024,128]{1,0:T(8,128)} %copy-done.1, f32[1024,128]{1,0:T(8,128)} %fusion.1.w_ref), custom_call_target="tpu_custom_call" | custom-call | tf_op jit(solution)/shard_map/pallas_call | solution.py:320
  412.6 17.5 %shard_map.70 = f32[1024,512]{1,0:T(8,128)} custom-call(f32[1024,128]{1,0:T(8,128)} %get-tuple-element.13.x_ref), custom_call_target="tpu_custom_call" | custom-call | flops 1000000 | bytes 40000000 | tf_op jit(solution)/shard_map/pallas_call | solution.py:261
  430.1 5.7 fusion.152.x_ref
  435.8 17.3 %shard_map.71.x_ref = f32[512,128]{1,0:T(8,128)} custom-call(f32[512,128]{1,0:T(8,128)} %fusion.152.x_ref), custom_call_target="tpu_custom_call" | custom-call | flops 1000000 | bytes 40000000 | tf_op jit(solution)/shard_map/pallas_call | solution.py:196
  453.1 11.2 %shard_map.72.margin_ref = f32[512,512]{1,0:T(8,128)} custom-call(f32[512,128]{1,0:T(8,128)} %shard_map.71.x_ref), custom_call_target="tpu_custom_call" | custom-call | flops 1000000 | bytes 40000000 | tf_op jit(solution)/shard_map/pallas_call | solution.py:261
  464.3 75.3 %shard_map.73 = f32[512,512]{1,0:T(8,128)} custom-call(f32[512,512]{1,0:T(8,128)} %shard_map.72.margin_ref), custom_call_target="tpu_custom_call" | custom-call | tf_op jit(solution)/shard_map/pallas_call | solution.py:123
  539.6 3.4 fusion.93.v_ref
  557.7 4.1 convolution_bitcast_fusion.3.x_ref
  561.8 24.2 %shard_map.74 = f32[512,128]{1,0:T(8,128)} custom-call(f32[512,128]{1,0:T(8,128)} %convolution_bitcast_fusion.3.x_ref), custom_call_target="tpu_custom_call" | custom-call | flops 1000000 | bytes 40000000 | tf_op jit(solution)/shard_map/pallas_call | solution.py:196
  588.1 3.8 multiply_add_fusion
  594.6 15.1 %shard_map.75 = (f32[1024,128]{1,0:T(8,128)}, f32[1,128]{1,0:T(1,128)}, f32[1,128]{1,0:T(1,128)}) custom-call(f32[1024,128]{1,0:T(8,128)} %copy-done, f32[1024,128]{1,0:T(8,128)} %fusion.2.w_ref), custom_call_target="tpu_custom_call" | custom-call | tf_op jit(solution)/shard_map/pallas_call | solution.py:320
  (135 shorter events, 47.3 us)
Async XLA Ops:
  7.2 19.6 %copy-start.5 = (f32[4,16,16,128]{3,2,1,0:T(8,128)S(1)}, f32[4,16,16,128]{3,2,1,0:T(8,128)}, u32[]{:S(2)}) copy-start(f32[4,16,16,128]{3,2,1,0:T(8,128)} %param.3) | copy-start | bytes 1572868
  7.2 164.4 %all-gather.2.cloned.1.call-start = ((), (), s32[]{:S(2)}) async-start(), calls=%async_computation | async-start | bytes 2621440 | tf_op jit(solution)/shard_map/all_gather | solution.py:335
  32.5 105.8 %copy-start.4 = (f32[1024,512]{1,0:T(8,128)S(1)}, f32[1024,512]{1,0:T(8,128)}, u32[]{:S(2)}) copy-start(f32[1024,512]{1,0:T(8,128)} %shard_map.58) | copy-start | bytes 6291460
  141.7 26.3 %copy-start.2 = (f32[128,1024]{0,1:T(8,128)}, f32[128,1024]{0,1:T(8,128)S(1)}, u32[]{:S(2)}) copy-start(f32[128,1024]{0,1:T(8,128)S(1)} %copy.6) | copy-start | bytes 1572868
  141.7 25.5 %collective-permute-start = (f32[4,16,16,128]{3,2,1,0:T(8,128)S(1)}, f32[4,16,16,128]{3,2,1,0:T(8,128)S(1)}, u32[]{:S(2)}, u32[]{:S(2)}) collective-permute-start(f32[4,16,16,128]{3,2,1,0:T(8,128)S(1)} %bitcast.88), channel_id=1, source_target_pairs={{4,0},{8,4},{12,8},{16,12},{20,16},{24,20},{28,24},{0,28},{5,1},{9... | collective-permute-start | bytes 1572872 | tf_op jit(solution)/shard_map/ppermute | solution.py:30
  146.5 20.8 %collective-permute-start.1 = (f32[4,16,16,128]{3,2,1,0:T(8,128)S(1)}, f32[4,16,16,128]{3,2,1,0:T(8,128)}, u32[]{:S(2)}, u32[]{:S(2)}) collective-permute-start(f32[4,16,16,128]{3,2,1,0:T(8,128)S(1)} %bitcast.89), channel_id=1, source_target_pairs={{0,4},{4,8},{8,12},{12,16},{16,20},{20,24},{24,28},{28,0},{1,5},{5... | collective-permute-start | bytes 1572872 | tf_op jit(solution)/shard_map/ppermute | solution.py:27
  147.7 20.3 %copy-start.29 = (f32[4,16,16]{2,1,0:T(8,128)S(1)}, f32[4,16,16]{2,1,0:T(8,128)}, u32[]{:S(2)}) copy-start(f32[4,16,16]{2,1,0:T(8,128)} %param.5) | copy-start | bytes 12292
  171.6 24.6 %copy-start.3 = (f32[4,16,16,512]{3,2,1,0:T(8,128)S(1)}, f32[4,16,16,512]{3,2,1,0:T(8,128)}, u32[]{:S(2)}) copy-start(f32[4,16,16,512]{3,2,1,0:T(8,128)} %all-gather.2.cloned.1.call-done) | copy-start | bytes 6291460
  215.4 17.5 %copy-start.16 = (f32[1024,128]{1,0:T(8,128)S(1)}, f32[1024,128]{1,0:T(8,128)}, u32[]{:S(2)}) copy-start(f32[1024,128]{1,0:T(8,128)} %get-tuple-element.12.x_ref) | copy-start | bytes 1572868
  345.7 43.2 %copy-start.1 = (f32[1024,128]{1,0:T(8,128)}, f32[1024,128]{1,0:T(8,128)S(1)}, u32[]{:S(2)}) copy-start(f32[1024,128]{1,0:T(8,128)S(1)} %fusion.95.v_ref) | copy-start | bytes 1572868
  351.6 37.3 %collective-permute-start.2 = (f32[4,16,16,128]{3,2,1,0:T(8,128)S(1)}, f32[4,16,16,128]{3,2,1,0:T(8,128)}, u32[]{:S(2)}, u32[]{:S(2)}) collective-permute-start(f32[4,16,16,128]{3,2,1,0:T(8,128)S(1)} %bitcast.75), channel_id=1, source_target_pairs={{4,0},{8,4},{12,8},{16,12},{20,16},{24,20},{28,24},{0,28},{5,1},{9... | collective-permute-start | bytes 1572872 | tf_op jit(solution)/shard_map/ppermute | solution.py:30
  354.7 34.2 %collective-permute-start.3 = (f32[4,16,16,128]{3,2,1,0:T(8,128)S(1)}, f32[4,16,16,128]{3,2,1,0:T(8,128)}, u32[]{:S(2)}, u32[]{:S(2)}) collective-permute-start(f32[4,16,16,128]{3,2,1,0:T(8,128)S(1)} %bitcast.76), channel_id=1, source_target_pairs={{0,4},{4,8},{8,12},{12,16},{16,20},{20,24},{24,28},{28,0},{1,5},{5... | collective-permute-start | bytes 1572872 | tf_op jit(solution)/shard_map/ppermute | solution.py:27
  388.7 1.6 copy-start.13
  388.7 1.8 copy-start.18
  388.7 1.9 copy-start.19
  388.7 2.0 copy-start.22
  388.7 2.0 copy-start.26
  390.8 4.0 copy-start.25
  412.6 17.5 %copy-start.17 = (f32[1024,128]{1,0:T(8,128)S(1)}, f32[1024,128]{1,0:T(8,128)}, u32[]{:S(2)}) copy-start(f32[1024,128]{1,0:T(8,128)} %get-tuple-element.13.x_ref) | copy-start | bytes 1572868
  543.0 43.3 %copy-start = (f32[1024,128]{1,0:T(8,128)}, f32[1024,128]{1,0:T(8,128)S(1)}, u32[]{:S(2)}) copy-start(f32[1024,128]{1,0:T(8,128)S(1)} %fusion.93.v_ref) | copy-start | bytes 1572868
  548.9 37.4 %collective-permute-start.4 = (f32[4,16,16,128]{3,2,1,0:T(8,128)S(1)}, f32[4,16,16,128]{3,2,1,0:T(8,128)}, u32[]{:S(2)}, u32[]{:S(2)}) collective-permute-start(f32[4,16,16,128]{3,2,1,0:T(8,128)S(1)} %bitcast.56), channel_id=1, source_target_pairs={{4,0},{8,4},{12,8},{16,12},{20,16},{24,20},{28,24},{0,28},{5,1},{9... | collective-permute-start | bytes 1572872 | tf_op jit(solution)/shard_map/ppermute | solution.py:30
  552.0 34.3 %collective-permute-start.5 = (f32[4,16,16,128]{3,2,1,0:T(8,128)S(1)}, f32[4,16,16,128]{3,2,1,0:T(8,128)}, u32[]{:S(2)}, u32[]{:S(2)}) collective-permute-start(f32[4,16,16,128]{3,2,1,0:T(8,128)S(1)} %bitcast.57), channel_id=1, source_target_pairs={{0,4},{4,8},{8,12},{12,16},{16,20},{20,24},{24,28},{28,0},{1,5},{5... | collective-permute-start | bytes 1572872 | tf_op jit(solution)/shard_map/ppermute | solution.py:27
  586.1 1.6 copy-start.15
  586.1 1.8 copy-start.20
  586.1 1.9 copy-start.21
  586.1 2.0 copy-start.23
  586.1 2.0 copy-start.27
  588.1 3.8 copy-start.24
  592.0 17.7 %copy-start.30 = (f32[1,128]{1,0:T(1,128)S(1)}, f32[1,128]{1,0:T(1,128)}, u32[]{:S(2)}) copy-start(f32[1,128]{1,0:T(1,128)} %get-tuple-element.15) | copy-start | bytes 1540
  592.0 17.7 %copy-start.31 = (f32[1,128]{1,0:T(1,128)S(1)}, f32[1,128]{1,0:T(1,128)}, u32[]{:S(2)}) copy-start(f32[1,128]{1,0:T(1,128)} %get-tuple-element.18) | copy-start | bytes 1540
  592.0 17.7 %copy-start.32 = (f32[1,128]{1,0:T(1,128)S(1)}, f32[1,128]{1,0:T(1,128)}, u32[]{:S(2)}) copy-start(f32[1,128]{1,0:T(1,128)} %get-tuple-element.16) | copy-start | bytes 1540
  592.0 17.7 %copy-start.33 = (f32[1,128]{1,0:T(1,128)S(1)}, f32[1,128]{1,0:T(1,128)}, u32[]{:S(2)}) copy-start(f32[1,128]{1,0:T(1,128)} %get-tuple-element.19) | copy-start | bytes 1540
  (9 other events, 10.9 us)
Sparse Core Ops, SparseCore 0:
  147.1 23.6 all-gather.1

commit v2 on v1

--- a/solution.py
+++ b/solution.py
@@ -18,26 +18,12 @@
 VMEM = pl.BlockSpec(memory_space=pltpu.VMEM)
 
 
-def with_halo(block, sides, width):
-    for axis, dim in sides:
-        count = lax.axis_size(axis)
-        forward = [(i, i + 1) for i in range(count - 1)]
-        forward.append((count - 1, 0))
-        backward = [(target, source) for source, target in forward]
-        low = lax.ppermute(
-            lax.slice_in_dim(block, block.shape[dim] - width, None, axis=dim), axis, forward
-        )
-        high = lax.ppermute(lax.slice_in_dim(block, 0, width, axis=dim), axis, backward)
-        block = jnp.concatenate([low, block, high], axis=dim)
-    return block
-
-
-def matmul(left, right):
-    return jnp.dot(left, right, precision=HIGHEST, preferred_element_type=jnp.float32)
-
-
-def laplacian(grid_field):
-    padded = with_halo(grid_field, (("grid", 0),), 4)
+def matmul(left, right, precision=HIGHEST):
+    return jnp.dot(left, right, precision=precision, preferred_element_type=jnp.float32)
+
+
+def laplacian(grid_field, low, high):
+    padded = jnp.concatenate([low, grid_field, high], axis=0)
     planes_here = grid_field.shape[0]
     result = 3.0 * STENCIL[0] * grid_field
     for distance in range(1, 5):
@@ -65,29 +51,44 @@
     groups = [block[8 * g : 8 * g + 8, :] for g in range(size // 8)]
     lane = lax.broadcasted_iota(jnp.int32, (8, size), 1)
     sublane = lax.broadcasted_iota(jnp.int32, (8, size), 0)
+
+    def spread_row(value, s):
+        return jnp.broadcast_to(value[s : s + 1, :], (8, size))
+
+    def spread_column(value, j):
+        return jnp.broadcast_to(value[:, j : j + 1], (8, size))
+
     finished = []
     for g in range(size // 8):
+        first = 8 * g
+        inside = (lane >= first) & (lane < first + 8)
+        columns = [spread_column(groups[g], first + t) for t in range(8)]
+        entry = [[spread_row(columns[t], s) for t in range(s + 1)] for s in range(8)]
+        start = jnp.where(inside, jnp.where(lane - first == sublane, 1.0, 0.0), groups[g])
+        rows = [spread_row(start, s) for s in range(8)]
+        inverse_pivot = []
+        factor = [[None] * 8 for _ in range(8)]
+        for t in range(8):
+            inverse_pivot.append(1.0 / entry[t][t])
+            for s in range(t + 1, 8):
+                factor[s][t] = entry[s][t] * inverse_pivot[t]
+                for u in range(t + 1, s + 1):
+                    entry[s][u] = entry[s][u] - factor[s][t] * entry[u][t]
+                rows[s] = rows[s] - factor[s][t] * rows[t]
         result = jnp.zeros((8, size), jnp.float32)
         for s in range(8):
-            j = 8 * g + s
-            row = jnp.broadcast_to(groups[g][s : s + 1, :], (8, size))
-            pivot = jnp.broadcast_to(row[:, j : j + 1], (8, size))
-            at_pivot = lane == j
-            row = jnp.where(at_pivot, 1.0, row)
-            scaled = row * (1.0 / pivot)
-            result = jnp.where(
-                (sublane == s) & (lane <= j), row * (1.0 / jnp.sqrt(pivot)), result
-            )
-            for i in range(g, size // 8):
-                column = jnp.broadcast_to(groups[i][:, j : j + 1], (8, size))
-                groups[i] = jnp.where(at_pivot, 0.0, groups[i]) - column * scaled if i > g else (
-                    jnp.where(
-                        sublane > s,
-                        jnp.where(at_pivot, 0.0, groups[i]) - column * scaled,
-                        groups[i],
-                    )
-                )
-        finished.append(result)
+            result = jnp.where(sublane == s, rows[s] * (1.0 / jnp.sqrt(entry[s][s])), result)
+        finished.append(jnp.where(lane < first + 8, result, 0.0))
+        solved = [None] * 8
+        for s in reversed(range(8)):
+            solved[s] = rows[s] * inverse_pivot[s]
+            for t in range(s + 1, 8):
+                solved[s] = solved[s] - factor[t][s] * solved[t]
+        for i in range(g + 1, size // 8):
+            value = jnp.where(inside, 0.0, groups[i])
+            for t in range(8):
+                value = value - spread_column(groups[i], first + t) * solved[t]
+            groups[i] = value
     return jnp.concatenate(finished, axis=0)
 
 
@@ -152,10 +153,41 @@
     )
 
 
-def grid_sum_kernel(count, x_ref, out_ref, parts, mine, total, s1, r1, s2, r2):
+def ring_places(count):
+    me = lax.axis_index("band")
+    half, side = lax.div(me, 2), lax.rem(me, 2)
+    partner = half * 2 + 1 - side
+    across = (1 - half) * 2 + side
+    return me, partner, across, (1 - half) * 2 + 1 - side
+
+
+def grid_sum_kernel(count, bands, edge, kind, *refs):
+    refs = list(refs)
+    x_ref = refs.pop(0)
+    extra = refs.pop(0) if kind else None
+    out_ref = refs.pop(0)
+    extra_out = [refs.pop(0) for _ in range({"": 0, "gather": 1, "halo": 2}[kind])]
+    parts, mine, total, s1, r1, s2, r2 = refs[:7]
     me = lax.axis_index("grid")
     chunk = x_ref.shape[0] // count
-    greet("grid", count, me)
+    barrier = pltpu.get_barrier_semaphore()
+    for k in range(1, count):
+        pl.semaphore_signal(
+            barrier, inc=1, device_id={"grid": lax.rem(me + k, count)}, device_id_type=MESH
+        )
+    greeted = count - 1
+    if kind == "gather":
+        place, partner, across, opposite = ring_places(bands)
+        for peer in (partner, across):
+            pl.semaphore_signal(barrier, inc=1, device_id={"band": peer}, device_id_type=MESH)
+        greeted += 2
+    pl.semaphore_wait(barrier, greeted)
+    if kind == "gather":
+        held, send, recv = refs[7:]
+        far = remote("band", across, extra, held.at[0], send.at[0], recv.at[0])
+        near = remote("band", partner, extra, held.at[1], send.at[1], recv.at[1])
+        far.start()
+        near.start()
     copies = []
     for k in range(1, count):
         peer = lax.rem(me + k, count)
@@ -169,6 +201,25 @@
         )
         copy.start()
         copies.append(copy)
+    if kind == "halo":
+        held, send, recv = refs[7:]
+        cells = extra.shape[0]
+        after = remote(
+            "grid",
+            lax.rem(me + 1, count),
+            extra.at[pl.ds(cells - edge, edge), :],
+            held.at[0],
+            send.at[0],
+            recv.at[0],
+        )
+        before = remote(
+            "grid",
+            lax.rem(me + count - 1, count),
+            extra.at[pl.ds(0, edge), :],
+            held.at[1],
+            send.at[1],
+            recv.at[1],
+        )
     own = pl.ds(pl.multiple_of(me * chunk, chunk), chunk)
     mine[...] = x_ref[own, :]
     for k in range(1, count):
@@ -181,23 +232,63 @@
         copy = remote("grid", peer, mine, total.at[me], s2.at[k - 1], r2.at[k - 1])
         copy.start()
         back.append(copy)
+    if kind == "halo":
+        after.start()
+        before.start()
+    if kind == "gather":
+        width = extra.shape[1]
+
+        def put(source, value):
+            extra_out[0][:, pl.ds(pl.multiple_of(source * width, width), width)] = value
+
+        far.wait_recv()
+        relay = remote("band", partner, held.at[0], held.at[2], send.at[2], recv.at[2])
+        relay.start()
+        put(place, extra[...])
+        near.wait_recv()
+        put(partner, held[1])
+        put(across, held[0])
+        relay.wait_recv()
+        put(opposite, held[2])
+        far.wait_send()
+        near.wait_send()
+        relay.wait_send()
     for k in range(1, count):
         copies[k - 1].wait_send()
         back[k - 1].wait()
     for c in range(count):
         out_ref[c * chunk : (c + 1) * chunk, :] = total[c]
-
-
-def grid_sum(x):
+    if kind == "halo":
+        after.wait()
+        before.wait()
+        extra_out[0][...] = held[0]
+        extra_out[1][...] = held[1]
+
+
+def grid_sum(x, collective, kind="", extra=None, edge=0):
     count = lax.axis_size("grid")
+    bands = lax.axis_size("band")
     rows, columns = x.shape
     chunk = rows // count
     sems = pltpu.SemaphoreType.DMA((count - 1,))
-    return pl.pallas_call(
-        functools.partial(grid_sum_kernel, count),
-        out_shape=jax.ShapeDtypeStruct(x.shape, jnp.float32),
-        in_specs=[VMEM],
-        out_specs=VMEM,
+    out_shape = [jax.ShapeDtypeStruct(x.shape, jnp.float32)]
+    more = []
+    if kind == "gather":
+        cells, width = extra.shape
+        out_shape.append(jax.ShapeDtypeStruct((cells, width * bands), jnp.float32))
+        more = [pltpu.VMEM((3, cells, width), jnp.float32)]
+        more += [pltpu.SemaphoreType.DMA((3,))] * 2
+    if kind == "halo":
+        width = extra.shape[1]
+        out_shape += [jax.ShapeDtypeStruct((edge, width), jnp.float32)] * 2
+        more = [pltpu.VMEM((2, edge, width), jnp.float32)]
+        more += [pltpu.SemaphoreType.DMA((2,))] * 2
+    operands = [x] + ([extra] if kind else [])
+    result = pl.pallas_call(
+        functools.partial(grid_sum_kernel, count, bands, edge, kind),
+        out_shape=out_shape,
+        in_specs=[VMEM] * len(operands),
+        out_specs=[VMEM] * len(out_shape),
         scratch_shapes=[
             pltpu.VMEM((count - 1, chunk, columns), jnp.float32),
             pltpu.VMEM((chunk, columns), jnp.float32),
@@ -206,10 +297,12 @@
             sems,
             sems,
             sems,
-        ],
-        compiler_params=pltpu.CompilerParams(collective_id=1, has_side_effects=True),
+        ]
+        + more,
+        compiler_params=pltpu.CompilerParams(collective_id=collective, has_side_effects=True),
         cost_estimate=pl.CostEstimate(flops=10**6, bytes_accessed=4 * 10**7, transcendentals=0),
-    )(x)
+    )(*operands)
+    return result
 
 
 def band_gather_kernel(count, x_ref, out_ref, held, send, recv):
@@ -332,14 +425,21 @@
     local_bands = orbitals.shape[3]
     first_band = lax.axis_index("band") * local_bands
     vectors = orbitals.reshape(-1, local_bands)
-    every_projector = lax.all_gather(projectors, "band", axis=3, tiled=True).reshape(
-        -1, projectors.shape[3] * lax.axis_size("band")
-    )
+    plane = vectors.shape[0] // grid_shape[0]
+    projector_rows = projectors.reshape(-1, projectors.shape[3])
+    joined = lax.axis_size("band") == 4
+    if not joined:
+        every_projector = band_gather(projector_rows, 3)
     quotient_list = []
     norm_list = []
     for iteration in range(ITERS):
         gathered = band_gather(vectors, 2)
-        margin = band_gather(grid_sum(matmul(gathered.T, vectors)), 3)
+        share = matmul(gathered.T, vectors)
+        if iteration == 0 and joined:
+            summed, every_projector = grid_sum(share, 5, "gather", projector_rows)
+        else:
+            (summed,) = grid_sum(share, 1)
+        margin = band_gather(summed, 6)
         inverse = inverse_factor(margin, local_bands)
         rows = lax.dynamic_slice_in_dim(inverse, first_band, local_bands, 0)
         vectors = lax.dot_general(
@@ -349,10 +449,14 @@
             precision=HIGHEST,
             preferred_element_type=jnp.float32,
         )
-        coupling = grid_sum(matmul(every_projector.T, vectors))
-        exchange_part = matmul(every_projector, coupling)
+        coupling, low, high = grid_sum(
+            matmul(every_projector.T, vectors, lax.Precision.HIGH), 7, "halo", vectors, 4 * plane
+        )
+        exchange_part = matmul(every_projector, coupling, lax.Precision.HIGH)
         grid_field = vectors.reshape(grid_shape)
-        applied = (-0.5 * laplacian(grid_field) + potential[..., None] * grid_field).reshape(
+        applied = (-0.5 * laplacian(
+            grid_field, low.reshape(4, *grid_shape[1:]), high.reshape(4, *grid_shape[1:])
+        ) + potential[..., None] * grid_field).reshape(
             -1, local_bands
         ) - exchange_part
         vectors, rayleigh, norm = update(vectors, applied)

time: 629 us -> 493 us (0.78)
  Pallas kernels: 481 us -> 397 us
  waiting for transfers between devices: 19.4 us -> 0 us
  between operations: 15.2 us -> 2.04 us
  starting transfers between devices: 11.4 us -> 0 us
  local copies, waits for them, and re-layouts: 30.9 us -> 40.7 us
  matrix products: 50.1 us -> 40.8 us
    pallas_call x3, Pallas kernels: 226 us -> 95.1 us  [inverse_factor(): pl.pallas_call(functools.partial(inverse_factor_kernel, size, block), out...]
    pallas_call x6, Pallas kernels: 121 us -> 172 us  [grid_sum(): pl.pallas_call(functools.partial(grid_sum_kernel, count, bands, edge, kin...]
    ppermute x6 -> x0, waiting for transfers between devices: 19.4 us -> none  [the longest x3 19.4 us: with_halo(): lax.ppermute(lax.slice_in_dim(block, 0, width, axis=dim), axis, backward)]
    ppermute x6 -> x0, starting transfers between devices: 11.4 us -> none  [the longest x3 10.9 us: with_halo(): lax.ppermute(lax.slice_in_dim(block, 0, width, axis=dim), axis, backward)]
    dot_general x9, matrix products: 40.1 us -> 30.1 us  [matmul(): jnp.dot(left, right, precision=precision, preferred_element_type=jnp.floa...]
    slice x48, local copies, waits for them, and re-layouts: 24.3 us -> 32.6 us  [laplacian(): jnp.roll(grid_field, distance, dimension)]
  transfers between devices with their start and end apart: 7 -> 0, of which waited for: 1 -> 0; matrix products, arithmetic and copies ran while one was open for 4% -> 0% of each run, Pallas kernels for 8% -> 0%
where the time goes in v2:
time: 493 us; the launch traced here: 489 us
  Pallas kernels  397 us (81%)
  matrix products  40.8 us (8%)
  local copies, waits for them, and re-layouts  40.7 us (8%)
  other arithmetic  8.19 us (2%)
    pallas_call x6, Pallas kernels, grid_sum(): pl.pallas_call(functools.partial(grid_sum_kernel, count, bands, edge, kin...  172 us
    pallas_call x3, Pallas kernels, inverse_factor(): pl.pallas_call(functools.partial(inverse_factor_kernel, size, block), out...  95.1 us
    pallas_call x6, Pallas kernels, band_gather(): pl.pallas_call(functools.partial(band_gather_kernel, count), out_shape=ja...  88.8 us
    pallas_call x3, Pallas kernels, update(): pl.pallas_call(functools.partial(update_kernel, count), out_shape=(jax.Sh...  41.4 us
    slice x48, local copies, waits for them, and re-layouts, laplacian(): jnp.roll(grid_field, distance, dimension)  32.6 us
    dot_general x9, matrix products, matmul(): jnp.dot(left, right, precision=precision, preferred_element_type=jnp.floa...  30.1 us
    dot_general x3, matrix products, local(): lax.dot_general(gathered, rows, (((1,), (1,)), ((), ())), precision=HIGHE...  10.7 us

profile of v2, /device:TPU:0, one launch (start us, length us, event | category | flops | bytes accessed | tf_op | source)
XLA Modules:
  0.0 488.9 jit_solution(149264133706544165)
XLA Ops:
  0.6 19.6 %shard_map.58 = f32[1024,512]{1,0:T(8,128)} custom-call(f32[1024,128]{1,0:T(8,128)} %bitcast.91), custom_call_target="tpu_custom_call" | custom-call | flops 1000000 | bytes 40000000 | tf_op jit(solution)/shard_map/pallas_call | solution.py:354
  20.2 5.7 %fusion.147.refs_0_ = f32[512,128]{1,0:T(8,128)} fusion(f32[1024,512]{1,0:T(8,128)} %shard_map.58, f32[1024,128]{1,0:T(8,128)S(1)} %bitcast.92), kind=kOutput, calls=%fused_computation.209 | convolution fusion | flops 805306368 | bytes 2883584 | tf_op jit(solution)/shard_map/dot_general | solution.py:22
  25.9 22.3 %shard_map.59 = (f32[512,128]{1,0:T(8,128)}, f32[1024,512]{1,0:T(8,128)}) custom-call(f32[512,128]{1,0:T(8,128)} %fusion.147.refs_0_, f32[1024,128]{1,0:T(8,128)} %bitcast.102), custom_call_target="tpu_custom_call" | custom-call | flops 1000000 | bytes 40000000 | tf_op jit(solution)/shard_map/pallas_call | solution.py:287
  48.3 11.8 %shard_map.60.margin_ref = f32[512,512]{1,0:T(8,128)} custom-call(f32[512,128]{1,0:T(8,128)} %get-tuple-element.23.x_ref), custom_call_target="tpu_custom_call" | custom-call | flops 1000000 | bytes 40000000 | tf_op jit(solution)/shard_map/pallas_call | solution.py:354
  60.1 31.9 %shard_map.61 = f32[512,512]{1,0:T(8,128)} custom-call(f32[512,512]{1,0:T(8,128)} %shard_map.60.margin_ref), custom_call_target="tpu_custom_call" | custom-call | tf_op jit(solution)/shard_map/pallas_call | solution.py:124
  92.0 3.9 fusion.94
  95.9 2.5 fusion.148.refs_0_
  108.0 37.0 %shard_map.62 = (f32[512,128]{1,0:T(8,128)}, f32[1024,128]{1,0:T(8,128)}, f32[1024,128]{1,0:T(8,128)}) custom-call(f32[512,128]{1,0:T(8,128)} %fusion.148.refs_0_, f32[1024,128]{1,0:T(8,128)} %bitcast.84), custom_call_target="tpu_custom_call" | custom-call | flops 1000000 | bytes 40000000 | tf_op jit(solution)/shard_map/pallas_call | solution.py:287
  148.8 2.7 multiply_add_fusion.2
  151.5 1.8 convolution_subtract_fusion.2.w_ref
  153.3 14.1 %shard_map.63 = (f32[1024,128]{1,0:T(8,128)}, f32[1,128]{1,0:T(1,128)}, f32[1,128]{1,0:T(1,128)}) custom-call(f32[1024,128]{1,0:T(8,128)} %bitcast.86, f32[1024,128]{1,0:T(8,128)} %convolution_subtract_fusion.2.w_ref), custom_call_target="tpu_custom_call" | custom-call | tf_op jit(solution)/shard_map/pallas_call | solution.py:413
  167.5 17.6 %shard_map.64 = f32[1024,512]{1,0:T(8,128)} custom-call(f32[1024,128]{1,0:T(8,128)} %get-tuple-element.28.x_ref), custom_call_target="tpu_custom_call" | custom-call | flops 1000000 | bytes 40000000 | tf_op jit(solution)/shard_map/pallas_call | solution.py:354
  185.1 5.7 %fusion.149.refs_0_ = f32[512,128]{1,0:T(8,128)} fusion(f32[1024,512]{1,0:T(8,128)} %shard_map.64, f32[1024,128]{1,0:T(8,128)S(1)} %copy-done.8), kind=kOutput, calls=%fused_computation.211 | convolution fusion | flops 805306368 | bytes 2883584 | tf_op jit(solution)/shard_map/dot_general | solution.py:22
  190.8 17.1 %shard_map.65.x_ref = f32[512,128]{1,0:T(8,128)} custom-call(f32[512,128]{1,0:T(8,128)} %fusion.149.refs_0_), custom_call_target="tpu_custom_call" | custom-call | flops 1000000 | bytes 40000000 | tf_op jit(solution)/shard_map/pallas_call | solution.py:287
  207.9 11.2 %shard_map.66.margin_ref = f32[512,512]{1,0:T(8,128)} custom-call(f32[512,128]{1,0:T(8,128)} %shard_map.65.x_ref), custom_call_target="tpu_custom_call" | custom-call | flops 1000000 | bytes 40000000 | tf_op jit(solution)/shard_map/pallas_call | solution.py:354
  219.0 31.6 %shard_map.67 = f32[512,512]{1,0:T(8,128)} custom-call(f32[512,512]{1,0:T(8,128)} %shard_map.66.margin_ref), custom_call_target="tpu_custom_call" | custom-call | tf_op jit(solution)/shard_map/pallas_call | solution.py:124
  250.6 3.4 fusion.92.refs_1_.v_ref
  257.4 2.5 fusion.150.refs_0_
  265.9 39.3 %shard_map.68 = (f32[512,128]{1,0:T(8,128)}, f32[1024,128]{1,0:T(8,128)}, f32[1024,128]{1,0:T(8,128)}) custom-call(f32[512,128]{1,0:T(8,128)} %fusion.150.refs_0_, f32[1024,128]{1,0:T(8,128)} %copy-done.2), custom_call_target="tpu_custom_call" | custom-call | flops 1000000 | bytes 40000000 | tf_op jit(solution)/shard_map/pallas_call | solution.py:287
  308.9 2.1 multiply_add_fusion.1
  312.9 13.7 %shard_map.69 = (f32[1024,128]{1,0:T(8,128)}, f32[1,128]{1,0:T(1,128)}, f32[1,128]{1,0:T(1,128)}) custom-call(f32[1024,128]{1,0:T(8,128)} %copy-done.2, f32[1024,128]{1,0:T(8,128)} %convolution_subtract_fusion.1.w_ref), custom_call_target="tpu_custom_call" | custom-call | tf_op jit(solution)/shard_map/pallas_call | solution.py:413
  326.6 17.6 %shard_map.70 = f32[1024,512]{1,0:T(8,128)} custom-call(f32[1024,128]{1,0:T(8,128)} %get-tuple-element.32.x_ref), custom_call_target="tpu_custom_call" | custom-call | flops 1000000 | bytes 40000000 | tf_op jit(solution)/shard_map/pallas_call | solution.py:354
  344.2 5.7 %fusion.151.refs_0_ = f32[512,128]{1,0:T(8,128)} fusion(f32[1024,512]{1,0:T(8,128)} %shard_map.70, f32[1024,128]{1,0:T(8,128)S(1)} %copy-done.9), kind=kOutput, calls=%fused_computation.213 | convolution fusion | flops 805306368 | bytes 2883584 | tf_op jit(solution)/shard_map/dot_general | solution.py:22
  349.9 16.9 %shard_map.71.x_ref = f32[512,128]{1,0:T(8,128)} custom-call(f32[512,128]{1,0:T(8,128)} %fusion.151.refs_0_), custom_call_target="tpu_custom_call" | custom-call | flops 1000000 | bytes 40000000 | tf_op jit(solution)/shard_map/pallas_call | solution.py:287
  366.8 11.2 %shard_map.72.margin_ref = f32[512,512]{1,0:T(8,128)} custom-call(f32[512,128]{1,0:T(8,128)} %shard_map.71.x_ref), custom_call_target="tpu_custom_call" | custom-call | flops 1000000 | bytes 40000000 | tf_op jit(solution)/shard_map/pallas_call | solution.py:354
  378.0 31.6 %shard_map.73 = f32[512,512]{1,0:T(8,128)} custom-call(f32[512,512]{1,0:T(8,128)} %shard_map.72.margin_ref), custom_call_target="tpu_custom_call" | custom-call | tf_op jit(solution)/shard_map/pallas_call | solution.py:124
  409.6 3.4 fusion.90.refs_1_.v_ref
  416.4 2.5 fusion.152.refs_0_
  424.9 39.2 %shard_map.74 = (f32[512,128]{1,0:T(8,128)}, f32[1024,128]{1,0:T(8,128)}, f32[1024,128]{1,0:T(8,128)}) custom-call(f32[512,128]{1,0:T(8,128)} %fusion.152.refs_0_, f32[1024,128]{1,0:T(8,128)} %copy-done), custom_call_target="tpu_custom_call" | custom-call | flops 1000000 | bytes 40000000 | tf_op jit(solution)/shard_map/pallas_call | solution.py:287
  467.9 2.1 multiply_add_fusion
  471.8 13.6 %shard_map.75 = (f32[1024,128]{1,0:T(8,128)}, f32[1,128]{1,0:T(1,128)}, f32[1,128]{1,0:T(1,128)}) custom-call(f32[1024,128]{1,0:T(8,128)} %copy-done, f32[1024,128]{1,0:T(8,128)} %convolution_subtract_fusion.w_ref), custom_call_target="tpu_custom_call" | custom-call | tf_op jit(solution)/shard_map/pallas_call | solution.py:413
  486.8 1.9 copy.8
  (236 shorter events, 43.7 us)
Async XLA Ops:
  0.6 19.6 %copy-start.7 = (f32[4,16,16,128]{3,2,1,0:T(8,128)S(1)}, f32[4,16,16,128]{3,2,1,0:T(8,128)}, u32[]{:S(2)}) copy-start(f32[4,16,16,128]{3,2,1,0:T(8,128)} %param.3) | copy-start | bytes 1572868
  60.1 35.8 %copy-start.6 = (f32[1024,512]{1,0:T(8,128)S(1)}, f32[1024,512]{1,0:T(8,128)}, u32[]{:S(2)}) copy-start(f32[1024,512]{1,0:T(8,128)} %get-tuple-element.24) | copy-start | bytes 6291460
  98.6 8.5 %copy-start.4 = (f32[128,1024]{0,1:T(8,128)}, f32[128,1024]{0,1:T(8,128)S(1)}, u32[]{:S(2)}) copy-start(f32[128,1024]{0,1:T(8,128)S(1)} %copy.6) | copy-start | bytes 1572868
  108.0 38.3 %copy-start.5 = (f32[128,1024]{0,1:T(8,128)S(1)}, f32[128,1024]{0,1:T(8,128)}, u32[]{:S(2)}) copy-start(f32[128,1024]{0,1:T(8,128)} %copy-done.4) | copy-start | bytes 1572868
  146.7 2.1 copy-start.46
  146.7 2.1 copy-start.56
  146.7 2.2 copy-start.57
  146.7 2.1 copy-start.58
  146.7 2.1 copy-start.80
  148.8 2.7 copy-start.74
  167.5 17.6 %copy-start.8 = (f32[1024,128]{1,0:T(8,128)S(1)}, f32[1024,128]{1,0:T(8,128)}, u32[]{:S(2)}) copy-start(f32[1024,128]{1,0:T(8,128)} %get-tuple-element.28.x_ref) | copy-start | bytes 1572868
  254.0 11.1 %copy-start.2 = (f32[1024,128]{1,0:T(8,128)}, f32[1024,128]{1,0:T(8,128)S(1)}, u32[]{:S(2)}) copy-start(f32[1024,128]{1,0:T(8,128)S(1)} %fusion.92.refs_1_.v_ref) | copy-start | bytes 1572868
  265.9 40.6 %copy-start.3 = (f32[1024,128]{1,0:T(8,128)S(1)}, f32[1024,128]{1,0:T(8,128)}, u32[]{:S(2)}) copy-start(f32[1024,128]{1,0:T(8,128)} %copy-done.2) | copy-start | bytes 1572868
  306.8 2.1 copy-start.48
  306.8 2.1 copy-start.52
  306.8 2.2 copy-start.53
  306.8 2.1 copy-start.59
  306.8 2.1 copy-start.76
  308.9 2.1 copy-start.75
  326.6 17.6 %copy-start.9 = (f32[1024,128]{1,0:T(8,128)S(1)}, f32[1024,128]{1,0:T(8,128)}, u32[]{:S(2)}) copy-start(f32[1024,128]{1,0:T(8,128)} %get-tuple-element.32.x_ref) | copy-start | bytes 1572868
  413.0 11.1 %copy-start = (f32[1024,128]{1,0:T(8,128)}, f32[1024,128]{1,0:T(8,128)S(1)}, u32[]{:S(2)}) copy-start(f32[1024,128]{1,0:T(8,128)S(1)} %fusion.90.refs_1_.v_ref) | copy-start | bytes 1572868
  424.9 40.5 %copy-start.1 = (f32[1024,128]{1,0:T(8,128)S(1)}, f32[1024,128]{1,0:T(8,128)}, u32[]{:S(2)}) copy-start(f32[1024,128]{1,0:T(8,128)} %copy-done) | copy-start | bytes 1572868
  465.7 2.1 copy-start.50
  465.7 2.1 copy-start.54
  465.7 2.2 copy-start.55
  465.7 2.1 copy-start.60
  465.7 2.1 copy-start.78
  467.9 2.1 copy-start.73
  470.0 15.5 %copy-start.88 = (f32[1,128]{1,0:T(1,128)S(1)}, f32[1,128]{1,0:T(1,128)}, u32[]{:S(2)}) copy-start(f32[1,128]{1,0:T(1,128)} %get-tuple-element.37) | copy-start | bytes 1540
  470.0 15.5 %copy-start.89 = (f32[1,128]{1,0:T(1,128)S(1)}, f32[1,128]{1,0:T(1,128)}, u32[]{:S(2)}) copy-start(f32[1,128]{1,0:T(1,128)} %get-tuple-element.40) | copy-start | bytes 1540
  470.0 15.5 %copy-start.90 = (f32[1,128]{1,0:T(1,128)S(1)}, f32[1,128]{1,0:T(1,128)}, u32[]{:S(2)}) copy-start(f32[1,128]{1,0:T(1,128)} %get-tuple-element.38) | copy-start | bytes 1540
  470.0 15.5 %copy-start.91 = (f32[1,128]{1,0:T(1,128)S(1)}, f32[1,128]{1,0:T(1,128)}, u32[]{:S(2)}) copy-start(f32[1,128]{1,0:T(1,128)} %get-tuple-element.41) | copy-start | bytes 1540
  (60 other events, 86.0 us)

commit v3 on v2

--- a/solution.py
+++ b/solution.py
@@ -220,6 +220,8 @@
             send.at[1],
             recv.at[1],
         )
+        after.start()
+        before.start()
     own = pl.ds(pl.multiple_of(me * chunk, chunk), chunk)
     mine[...] = x_ref[own, :]
     for k in range(1, count):
@@ -232,9 +234,6 @@
         copy = remote("grid", peer, mine, total.at[me], s2.at[k - 1], r2.at[k - 1])
         copy.start()
         back.append(copy)
-    if kind == "halo":
-        after.start()
-        before.start()
     if kind == "gather":
         width = extra.shape[1]
 

time: 493 us -> 483 us (0.980)
  Pallas kernels: 397 us -> 387 us
    pallas_call x6, Pallas kernels: 172 us -> 165 us  [grid_sum(): pl.pallas_call(functools.partial(grid_sum_kernel, count, bands, edge, kin...]
where the time goes in v3:
time: 483 us; the launch traced here: 478 us
  Pallas kernels  387 us (80%)
  matrix products  40.8 us (8%)
  local copies, waits for them, and re-layouts  40.7 us (8%)
  other arithmetic  8.19 us (2%)
    pallas_call x6, Pallas kernels, grid_sum(): pl.pallas_call(functools.partial(grid_sum_kernel, count, bands, edge, kin...  165 us
    pallas_call x3, Pallas kernels, inverse_factor(): pl.pallas_call(functools.partial(inverse_factor_kernel, size, block), out...  95.1 us
    pallas_call x6, Pallas kernels, band_gather(): pl.pallas_call(functools.partial(band_gather_kernel, count), out_shape=ja...  88.8 us
    pallas_call x3, Pallas kernels, update(): pl.pallas_call(functools.partial(update_kernel, count), out_shape=(jax.Sh...  37.4 us
    slice x48, local copies, waits for them, and re-layouts, laplacian(): jnp.roll(grid_field, distance, dimension)  32.6 us
    dot_general x9, matrix products, matmul(): jnp.dot(left, right, precision=precision, preferred_element_type=jnp.floa...  30.1 us
    dot_general x3, matrix products, local(): lax.dot_general(gathered, rows, (((1,), (1,)), ((), ())), precision=HIGHE...  10.7 us

profile of v3, /device:TPU:0, one launch (start us, length us, event | category | flops | bytes accessed | tf_op | source)
XLA Modules:
  0.0 478.4 jit_solution(7641901541908655838)
XLA Ops:
  0.6 19.6 %shard_map.58 = f32[1024,512]{1,0:T(8,128)} custom-call(f32[1024,128]{1,0:T(8,128)} %bitcast.91), custom_call_target="tpu_custom_call" | custom-call | flops 1000000 | bytes 40000000 | tf_op jit(solution)/shard_map/pallas_call | solution.py:353
  20.2 5.7 %fusion.147.refs_0_ = f32[512,128]{1,0:T(8,128)} fusion(f32[1024,512]{1,0:T(8,128)} %shard_map.58, f32[1024,128]{1,0:T(8,128)S(1)} %bitcast.92), kind=kOutput, calls=%fused_computation.209 | convolution fusion | flops 805306368 | bytes 2883584 | tf_op jit(solution)/shard_map/dot_general | solution.py:22
  25.9 22.3 %shard_map.59 = (f32[512,128]{1,0:T(8,128)}, f32[1024,512]{1,0:T(8,128)}) custom-call(f32[512,128]{1,0:T(8,128)} %fusion.147.refs_0_, f32[1024,128]{1,0:T(8,128)} %bitcast.102), custom_call_target="tpu_custom_call" | custom-call | flops 1000000 | bytes 40000000 | tf_op jit(solution)/shard_map/pallas_call | solution.py:286
  48.3 11.8 %shard_map.60.margin_ref = f32[512,512]{1,0:T(8,128)} custom-call(f32[512,128]{1,0:T(8,128)} %get-tuple-element.23.x_ref), custom_call_target="tpu_custom_call" | custom-call | flops 1000000 | bytes 40000000 | tf_op jit(solution)/shard_map/pallas_call | solution.py:353
  60.1 31.9 %shard_map.61 = f32[512,512]{1,0:T(8,128)} custom-call(f32[512,512]{1,0:T(8,128)} %shard_map.60.margin_ref), custom_call_target="tpu_custom_call" | custom-call | tf_op jit(solution)/shard_map/pallas_call | solution.py:124
  92.0 3.9 fusion.94
  95.9 2.5 fusion.148.refs_0_
  108.0 34.8 %shard_map.62 = (f32[512,128]{1,0:T(8,128)}, f32[1024,128]{1,0:T(8,128)}, f32[1024,128]{1,0:T(8,128)}) custom-call(f32[512,128]{1,0:T(8,128)} %fusion.148.refs_0_, f32[1024,128]{1,0:T(8,128)} %bitcast.84), custom_call_target="tpu_custom_call" | custom-call | flops 1000000 | bytes 40000000 | tf_op jit(solution)/shard_map/pallas_call | solution.py:286
  146.6 2.7 multiply_add_fusion.2
  149.3 1.8 convolution_subtract_fusion.2.w_ref
  151.1 12.9 %shard_map.63 = (f32[1024,128]{1,0:T(8,128)}, f32[1,128]{1,0:T(1,128)}, f32[1,128]{1,0:T(1,128)}) custom-call(f32[1024,128]{1,0:T(8,128)} %bitcast.86, f32[1024,128]{1,0:T(8,128)} %convolution_subtract_fusion.2.w_ref), custom_call_target="tpu_custom_call" | custom-call | tf_op jit(solution)/shard_map/pallas_call | solution.py:412
  164.0 17.6 %shard_map.64 = f32[1024,512]{1,0:T(8,128)} custom-call(f32[1024,128]{1,0:T(8,128)} %get-tuple-element.28.x_ref), custom_call_target="tpu_custom_call" | custom-call | flops 1000000 | bytes 40000000 | tf_op jit(solution)/shard_map/pallas_call | solution.py:353
  181.6 5.7 %fusion.149.refs_0_ = f32[512,128]{1,0:T(8,128)} fusion(f32[1024,512]{1,0:T(8,128)} %shard_map.64, f32[1024,128]{1,0:T(8,128)S(1)} %copy-done.8), kind=kOutput, calls=%fused_computation.211 | convolution fusion | flops 805306368 | bytes 2883584 | tf_op jit(solution)/shard_map/dot_general | solution.py:22
  187.3 17.3 %shard_map.65.x_ref = f32[512,128]{1,0:T(8,128)} custom-call(f32[512,128]{1,0:T(8,128)} %fusion.149.refs_0_), custom_call_target="tpu_custom_call" | custom-call | flops 1000000 | bytes 40000000 | tf_op jit(solution)/shard_map/pallas_call | solution.py:286
  204.6 11.2 %shard_map.66.margin_ref = f32[512,512]{1,0:T(8,128)} custom-call(f32[512,128]{1,0:T(8,128)} %shard_map.65.x_ref), custom_call_target="tpu_custom_call" | custom-call | flops 1000000 | bytes 40000000 | tf_op jit(solution)/shard_map/pallas_call | solution.py:353
  215.8 31.6 %shard_map.67 = f32[512,512]{1,0:T(8,128)} custom-call(f32[512,512]{1,0:T(8,128)} %shard_map.66.margin_ref), custom_call_target="tpu_custom_call" | custom-call | tf_op jit(solution)/shard_map/pallas_call | solution.py:124
  247.3 3.4 fusion.92.refs_1_.v_ref
  254.1 2.5 fusion.150.refs_0_
  262.6 36.5 %shard_map.68 = (f32[512,128]{1,0:T(8,128)}, f32[1024,128]{1,0:T(8,128)}, f32[1024,128]{1,0:T(8,128)}) custom-call(f32[512,128]{1,0:T(8,128)} %fusion.150.refs_0_, f32[1024,128]{1,0:T(8,128)} %copy-done.2), custom_call_target="tpu_custom_call" | custom-call | flops 1000000 | bytes 40000000 | tf_op jit(solution)/shard_map/pallas_call | solution.py:286
  302.9 2.1 multiply_add_fusion.1
  306.9 12.6 %shard_map.69 = (f32[1024,128]{1,0:T(8,128)}, f32[1,128]{1,0:T(1,128)}, f32[1,128]{1,0:T(1,128)}) custom-call(f32[1024,128]{1,0:T(8,128)} %copy-done.2, f32[1024,128]{1,0:T(8,128)} %convolution_subtract_fusion.1.w_ref), custom_call_target="tpu_custom_call" | custom-call | tf_op jit(solution)/shard_map/pallas_call | solution.py:412
  319.5 17.6 %shard_map.70 = f32[1024,512]{1,0:T(8,128)} custom-call(f32[1024,128]{1,0:T(8,128)} %get-tuple-element.32.x_ref), custom_call_target="tpu_custom_call" | custom-call | flops 1000000 | bytes 40000000 | tf_op jit(solution)/shard_map/pallas_call | solution.py:353
  337.0 5.7 %fusion.151.refs_0_ = f32[512,128]{1,0:T(8,128)} fusion(f32[1024,512]{1,0:T(8,128)} %shard_map.70, f32[1024,128]{1,0:T(8,128)S(1)} %copy-done.9), kind=kOutput, calls=%fused_computation.213 | convolution fusion | flops 805306368 | bytes 2883584 | tf_op jit(solution)/shard_map/dot_general | solution.py:22
  342.8 17.6 %shard_map.71.x_ref = f32[512,128]{1,0:T(8,128)} custom-call(f32[512,128]{1,0:T(8,128)} %fusion.151.refs_0_), custom_call_target="tpu_custom_call" | custom-call | flops 1000000 | bytes 40000000 | tf_op jit(solution)/shard_map/pallas_call | solution.py:286
  360.4 11.2 %shard_map.72.margin_ref = f32[512,512]{1,0:T(8,128)} custom-call(f32[512,128]{1,0:T(8,128)} %shard_map.71.x_ref), custom_call_target="tpu_custom_call" | custom-call | flops 1000000 | bytes 40000000 | tf_op jit(solution)/shard_map/pallas_call | solution.py:353
  371.6 31.6 %shard_map.73 = f32[512,512]{1,0:T(8,128)} custom-call(f32[512,512]{1,0:T(8,128)} %shard_map.72.margin_ref), custom_call_target="tpu_custom_call" | custom-call | tf_op jit(solution)/shard_map/pallas_call | solution.py:124
  403.2 3.4 fusion.90.refs_1_.v_ref
  410.0 2.5 fusion.152.refs_0_
  418.5 36.8 %shard_map.74 = (f32[512,128]{1,0:T(8,128)}, f32[1024,128]{1,0:T(8,128)}, f32[1024,128]{1,0:T(8,128)}) custom-call(f32[512,128]{1,0:T(8,128)} %fusion.152.refs_0_, f32[1024,128]{1,0:T(8,128)} %copy-done), custom_call_target="tpu_custom_call" | custom-call | flops 1000000 | bytes 40000000 | tf_op jit(solution)/shard_map/pallas_call | solution.py:286
  459.1 2.1 multiply_add_fusion
  463.1 11.9 %shard_map.75 = (f32[1024,128]{1,0:T(8,128)}, f32[1,128]{1,0:T(1,128)}, f32[1,128]{1,0:T(1,128)}) custom-call(f32[1024,128]{1,0:T(8,128)} %copy-done, f32[1024,128]{1,0:T(8,128)} %convolution_subtract_fusion.w_ref), custom_call_target="tpu_custom_call" | custom-call | tf_op jit(solution)/shard_map/pallas_call | solution.py:412
  476.3 1.9 copy.8
  (236 shorter events, 43.7 us)
Async XLA Ops:
  0.6 19.6 %copy-start.7 = (f32[4,16,16,128]{3,2,1,0:T(8,128)S(1)}, f32[4,16,16,128]{3,2,1,0:T(8,128)}, u32[]{:S(2)}) copy-start(f32[4,16,16,128]{3,2,1,0:T(8,128)} %param.3) | copy-start | bytes 1572868
  60.1 35.8 %copy-start.6 = (f32[1024,512]{1,0:T(8,128)S(1)}, f32[1024,512]{1,0:T(8,128)}, u32[]{:S(2)}) copy-start(f32[1024,512]{1,0:T(8,128)} %get-tuple-element.24) | copy-start | bytes 6291460
  98.6 8.5 %copy-start.4 = (f32[128,1024]{0,1:T(8,128)}, f32[128,1024]{0,1:T(8,128)S(1)}, u32[]{:S(2)}) copy-start(f32[128,1024]{0,1:T(8,128)S(1)} %copy.6) | copy-start | bytes 1572868
  108.0 36.1 %copy-start.5 = (f32[128,1024]{0,1:T(8,128)S(1)}, f32[128,1024]{0,1:T(8,128)}, u32[]{:S(2)}) copy-start(f32[128,1024]{0,1:T(8,128)} %copy-done.4) | copy-start | bytes 1572868
  144.4 2.1 copy-start.46
  144.4 2.1 copy-start.56
  144.4 2.2 copy-start.57
  144.4 2.1 copy-start.58
  144.4 2.1 copy-start.80
  146.6 2.7 copy-start.74
  164.0 17.6 %copy-start.8 = (f32[1024,128]{1,0:T(8,128)S(1)}, f32[1024,128]{1,0:T(8,128)}, u32[]{:S(2)}) copy-start(f32[1024,128]{1,0:T(8,128)} %get-tuple-element.28.x_ref) | copy-start | bytes 1572868
  250.7 11.1 %copy-start.2 = (f32[1024,128]{1,0:T(8,128)}, f32[1024,128]{1,0:T(8,128)S(1)}, u32[]{:S(2)}) copy-start(f32[1024,128]{1,0:T(8,128)S(1)} %fusion.92.refs_1_.v_ref) | copy-start | bytes 1572868
  262.6 37.8 %copy-start.3 = (f32[1024,128]{1,0:T(8,128)S(1)}, f32[1024,128]{1,0:T(8,128)}, u32[]{:S(2)}) copy-start(f32[1024,128]{1,0:T(8,128)} %copy-done.2) | copy-start | bytes 1572868
  300.7 2.1 copy-start.48
  300.7 2.1 copy-start.52
  300.7 2.2 copy-start.53
  300.8 2.1 copy-start.59
  300.8 2.1 copy-start.76
  302.9 2.1 copy-start.75
  319.4 17.6 %copy-start.9 = (f32[1024,128]{1,0:T(8,128)S(1)}, f32[1024,128]{1,0:T(8,128)}, u32[]{:S(2)}) copy-start(f32[1024,128]{1,0:T(8,128)} %get-tuple-element.32.x_ref) | copy-start | bytes 1572868
  406.6 11.1 %copy-start = (f32[1024,128]{1,0:T(8,128)}, f32[1024,128]{1,0:T(8,128)S(1)}, u32[]{:S(2)}) copy-start(f32[1024,128]{1,0:T(8,128)S(1)} %fusion.90.refs_1_.v_ref) | copy-start | bytes 1572868
  418.5 38.1 %copy-start.1 = (f32[1024,128]{1,0:T(8,128)S(1)}, f32[1024,128]{1,0:T(8,128)}, u32[]{:S(2)}) copy-start(f32[1024,128]{1,0:T(8,128)} %copy-done) | copy-start | bytes 1572868
  456.9 2.1 copy-start.50
  456.9 2.1 copy-start.54
  456.9 2.2 copy-start.55
  456.9 2.1 copy-start.60
  456.9 2.1 copy-start.78
  459.1 2.1 copy-start.73
  461.2 13.7 %copy-start.88 = (f32[1,128]{1,0:T(1,128)S(1)}, f32[1,128]{1,0:T(1,128)}, u32[]{:S(2)}) copy-start(f32[1,128]{1,0:T(1,128)} %get-tuple-element.37) | copy-start | bytes 1540
  461.2 13.7 %copy-start.89 = (f32[1,128]{1,0:T(1,128)S(1)}, f32[1,128]{1,0:T(1,128)}, u32[]{:S(2)}) copy-start(f32[1,128]{1,0:T(1,128)} %get-tuple-element.40) | copy-start | bytes 1540
  461.2 13.7 %copy-start.90 = (f32[1,128]{1,0:T(1,128)S(1)}, f32[1,128]{1,0:T(1,128)}, u32[]{:S(2)}) copy-start(f32[1,128]{1,0:T(1,128)} %get-tuple-element.38) | copy-start | bytes 1540
  461.2 13.7 %copy-start.91 = (f32[1,128]{1,0:T(1,128)S(1)}, f32[1,128]{1,0:T(1,128)}, u32[]{:S(2)}) copy-start(f32[1,128]{1,0:T(1,128)} %get-tuple-element.41) | copy-start | bytes 1540
  (60 other events, 86.0 us)
